TPU v7x, 32 devices: a 4x4x1 block of a 4x4x8 slice. The times are simulated.
32 devices in a mesh: dp: 1 (over z), sp: 4 (over y), tp: 8 (over x, core).
Axes of the slice: x: 4, y: 4, z: 1, core: 2. Of those that a mesh axis runs over, the one named last changes fastest.
The devices are a block of a 4x4x8 slice.
Arguments:
- x: bfloat16 [8192, 2560], P(('dp', 'sp', 'tp'))
- segment_ids: int32 [8192], P(('dp', 'sp', 'tp'))
- positions: int32 [8192], P(('dp', 'sp', 'tp'))
- g_attn: bfloat16 [2, 2560], replicated
- w_q: bfloat16 [2, 2560, 8, 256], P(None, None, 'tp')
- w_k: bfloat16 [2, 2560, 4, 256], replicated
- w_v: bfloat16 [2, 2560, 4, 256], replicated
- w_o: bfloat16 [2, 8, 256, 2560], P(None, 'tp')
- g_mlp: bfloat16 [2, 2560], replicated
- w_gate: bfloat16 [2, 2560, 10240], P(None, None, 'tp')
- w_up: bfloat16 [2, 2560, 10240], P(None, None, 'tp')
- w_down: bfloat16 [2, 10240, 2560], P(None, 'tp')
Outputs:
- output: bfloat16 [8192, 2560], P(('dp', 'sp', 'tp'))
All inputs are finite; a program needn't handle non-finite values.
Results may differ from a plain program's by a relative error of at most 0.0197739.
Values are sent between devices in bfloat16 or wider.
A program may use at most 768 MiB of HBM per device.

v0:
```python
import jax
import jax.numpy as jnp
from jax import lax
from jax.sharding import PartitionSpec as P

EPS = 1e-6
ROPE_BASE = 10000.0
WINDOW = 1024
SCORE_ROWS = 256


def rms_norm(x, gain):
    x_wide = x.astype(jnp.float32)
    inv_rms = lax.rsqrt(jnp.mean(x_wide * x_wide, axis=-1, keepdims=True) + EPS)
    return (x_wide * inv_rms * gain.astype(jnp.float32)).astype(jnp.bfloat16)


def rope_tables(positions, head_dim):
    half_width = head_dim // 2
    inv_freq = ROPE_BASE ** (-jnp.arange(half_width, dtype=jnp.float32) / half_width)
    angles = positions.astype(jnp.float32)[:, None] * inv_freq[None, :]
    return jnp.cos(angles)[:, None, :], jnp.sin(angles)[:, None, :]


def rope(t, cos_tab, sin_tab):
    half_width = t.shape[-1] // 2
    t_wide = t.astype(jnp.float32)
    lower_half = t_wide[..., :half_width]
    upper_half = t_wide[..., half_width:]
    return jnp.concatenate([lower_half * cos_tab - upper_half * sin_tab, upper_half * cos_tab + lower_half * sin_tab], axis=-1).astype(jnp.bfloat16)


def attend(q, k_all, v_all, seg_q, seg_all, q_offset, windowed):
    q_rows, kv_count, group_size, head_dim = q.shape
    total = k_all.shape[0]
    block_rows = min(q_rows, max(SCORE_ROWS // (kv_count * group_size), 8))
    blocks = q_rows // block_rows
    key_span = min(block_rows + WINDOW, total) if windowed else total
    q_blocks = q.reshape(blocks, block_rows, kv_count, group_size, head_dim)
    seg_blocks = seg_q.reshape(blocks, block_rows)

    def one_block(block_args):
        q_blk, seg_blk, block_idx = block_args
        q_start = q_offset + block_idx * block_rows
        k_start = jnp.clip(q_start + block_rows - key_span, 0, total - key_span)
        k_blk = lax.dynamic_slice_in_dim(k_all, k_start, key_span, 0)
        v_blk = lax.dynamic_slice_in_dim(v_all, k_start, key_span, 0)
        seg_k = lax.dynamic_slice_in_dim(seg_all, k_start, key_span, 0)
        q_pos = q_start + jnp.arange(block_rows)
        k_pos = k_start + jnp.arange(key_span)
        allowed = (k_pos[None, :] <= q_pos[:, None]) & (seg_k[None, :] == seg_blk[:, None])
        if windowed:
            allowed = allowed & (q_pos[:, None] - k_pos[None, :] < WINDOW)
        scores = jnp.einsum("qgrd,kgd->qgrk", q_blk, k_blk, preferred_element_type=jnp.float32) * head_dim ** -0.5
        scores = jnp.where(allowed[:, None, None, :], scores, -1e30)
        attn_probs = jax.nn.softmax(scores, axis=-1).astype(jnp.bfloat16)
        return jnp.einsum("qgrk,kgd->qgrd", attn_probs, v_blk, preferred_element_type=jnp.float32).astype(jnp.bfloat16)

    out_blocks = lax.map(one_block, (q_blocks, seg_blocks, jnp.arange(blocks)))
    return out_blocks.reshape(q_rows, kv_count * group_size * head_dim)


def matmul(rows_in, weight):
    return jnp.dot(rows_in, weight, preferred_element_type=jnp.float32)


def solution(mesh):
    tp_size = mesh.shape["tp"]
    row_spec = P(("dp", "sp", "tp"), None)
    id_spec = P(("dp", "sp", "tp"))
    whole = P()
    in_specs = (row_spec, id_spec, id_spec, whole, P(None, None, "tp", None), whole, whole, P(None, "tp", None, None), whole, P(None, None, "tp"), P(None, None, "tp"), P(None, "tp", None))

    def local_fn(x, segment_ids, positions, g_attn, w_q, w_k, w_v, w_o, g_mlp, w_gate, w_up, w_down):
        sp_idx = lax.axis_index("sp")
        tp_idx = lax.axis_index("tp")
        layers, model, heads_loc, head_dim = w_q.shape
        kv_heads = w_k.shape[2]
        kv_loc = max(kv_heads // tp_size, 1)
        group_size = heads_loc // kv_loc
        kv_start = tp_idx * kv_heads // tp_size
        seg_all = lax.all_gather(segment_ids, ("sp", "tp"), tiled=True)
        pos_shard = lax.all_gather(positions, "tp", tiled=True)
        shard_rows = pos_shard.shape[0]
        q_offset = sp_idx * shard_rows
        seg_q = lax.dynamic_slice_in_dim(seg_all, q_offset, shard_rows, 0)
        cos_tab, sin_tab = rope_tables(pos_shard, head_dim)
        for layer in range(layers):
            normed = lax.all_gather(rms_norm(x, g_attn[layer]), "tp", tiled=True)
            w_k_loc = lax.dynamic_slice_in_dim(w_k[layer], kv_start, kv_loc, 1).reshape(model, kv_loc * head_dim)
            w_v_loc = lax.dynamic_slice_in_dim(w_v[layer], kv_start, kv_loc, 1).reshape(model, kv_loc * head_dim)
            q = matmul(normed, w_q[layer].reshape(model, heads_loc * head_dim)).astype(jnp.bfloat16)
            k = matmul(normed, w_k_loc).astype(jnp.bfloat16)
            v = matmul(normed, w_v_loc).astype(jnp.bfloat16)
            q = rope(q.reshape(shard_rows, heads_loc, head_dim), cos_tab, sin_tab).reshape(shard_rows, kv_loc, group_size, head_dim)
            k = rope(k.reshape(shard_rows, kv_loc, head_dim), cos_tab, sin_tab)
            k_all = lax.all_gather(k, "sp", tiled=True)
            v_all = lax.all_gather(v.reshape(shard_rows, kv_loc, head_dim), "sp", tiled=True)
            mixed = attend(q, k_all, v_all, seg_q, seg_all, q_offset, layer % 2 == 0)
            part_sum = matmul(mixed, w_o[layer].reshape(heads_loc * head_dim, model)).astype(jnp.bfloat16)
            attn_out = lax.psum_scatter(part_sum, "tp", scatter_dimension=0, tiled=True)
            hidden = (x.astype(jnp.float32) + attn_out.astype(jnp.float32)).astype(jnp.bfloat16)
            normed = lax.all_gather(rms_norm(hidden, g_mlp[layer]), "tp", tiled=True)
            activation = (jax.nn.silu(matmul(normed, w_gate[layer])) * matmul(normed, w_up[layer])).astype(jnp.bfloat16)
            part_sum = matmul(activation, w_down[layer]).astype(jnp.bfloat16)
            mlp_out = lax.psum_scatter(part_sum, "tp", scatter_dimension=0, tiled=True)
            x = (hidden.astype(jnp.float32) + mlp_out.astype(jnp.float32)).astype(jnp.bfloat16)
        return x

    return jax.shard_map(local_fn, mesh=mesh, in_specs=in_specs, out_specs=row_spec, check_vma=False)
```

profile of v0, /device:TPU:112, one launch (start us, length us, event | category | flops | bytes accessed | tf_op | source)
XLA Modules:
  0.0 978.2 jit_solution(12332302480363581566)
XLA Ops:
  12.0 23.6 %all-gather.3 = s32[8,1,256]{2,1,0:T(1,128)S(1)} all-gather(s32[1,1,256]{2,1,0:T(1,128)S(1)} %bitcast.207), channel_id=1, replica_groups=mesh['dp'=1,'sp'=4,'tp'=8] {'tp'}, dimensions={0}, use_global_device_ids=true | all-gather | bytes 9216 | tf_op jit(solution)/shard_map/all_gather | solution.py:83
  35.6 9.3 fusion.121
  47.7 22.1 %all-gather.13.cloned.1.call-done = bf16[2048,2560]{1,0:T(8,128)(2,1)} async-done(((bf16[256,2560]{1,0:T(8,128)(2,1)}), bf16[2048,2560]{1,0:T(8,128)(2,1)}) %all-gather.13.cloned.1.call-update) | async-done | bytes 10485776 | tf_op jit(solution)/shard_map/all_gather | solution.py:89
  69.9 6.0 fusion.72
  87.6 9.4 fusion.120
  99.7 7.9 convolution_convert_fusion.10
  107.7 32.4 %all-gather.2 = s32[32,1,256]{2,1,0:T(1,128)S(1)} all-gather(s32[1,1,256]{2,1,0:T(1,128)S(1)} %bitcast.208), channel_id=1, replica_groups=mesh['dp'=1,'sp'=4,'tp'=8] {'sp','tp'}, dimensions={0}, use_global_device_ids=true | all-gather | bytes 33792 | tf_op jit(solution)/shard_map/all_gather | solution.py:82
  141.8 38.5 %all-gather.25.cloned.1.call-done = bf16[8192,256]{1,0:T(8,128)(2,1)} async-done(((bf16[2048,256]{1,0:T(8,128)(2,1)}), bf16[8192,256]{1,0:T(8,128)(2,1)}) %all-gather.25.cloned.1.call-update) | async-done | bytes 4194320 | tf_op jit(solution)/shard_map/all_gather | solution.py:98
  180.4 51.7 %while.28 = (s32[]{:T(128)}, bf16[8,256,1,1,256]{4,1,0,3,2:T(8,128)(2,1)}, s32[8]{0:T(128)S(1)}, s32[]{:T(128)}, bf16[8192,1,256]{2,0,1:T(8,128)(2,1)}, /*index=...) while((s32[]{:T(128)}, ...), condition=%wide.region_4.5_spmd, body=%wide.region_1.4_spmd.sunk | while | flops 340198400 | bytes 6065397 | solution.py:59
  232.1 6.8 convolution_convert_fusion.4
  240.2 60.0 %reduce-scatter.5.cloned.1.call-done = bf16[256,2560]{1,0:T(8,128)(2,1)} async-done(((bf16[2048,2560]{1,0:T(8,128)(2,1)}), bf16[256,2560]{1,0:T(8,128)(2,1)}) %reduce-scatter.5.cloned.1.call-update) | async-done | bytes 1310736 | tf_op jit(solution)/shard_map/reduce_scatter | solution.py:101
  304.0 55.6 %all-gather.17.cloned.1.call-done = bf16[2048,2560]{1,0:T(8,128)(2,1)} async-done(((bf16[256,2560]{1,0:T(8,128)(2,1)}), bf16[2048,2560]{1,0:T(8,128)(2,1)}) %all-gather.17.cloned.1.call-update) | async-done | bytes 10485776 | tf_op jit(solution)/shard_map/all_gather | solution.py:103
  359.6 19.3 %fusion.45 = f32[2048,1280]{1,0:T(8,128)} fusion(bf16[2048,2560]{1,0:T(8,128)(2,1)} %all-gather.17.cloned.1.call-done, bf16[2,2560,1280]{2,1,0:T(8,128)(2,1)} %param.25), kind=kOutput, calls=%fused_computation.54 | convolution fusion | flops 13421772800 | bytes 27525120 | tf_op jit(solution)/shard_map/dot_general | solution.py:64
  379.0 19.5 %multiply_convert_fusion.1 = bf16[2048,1280]{1,0:T(8,128)(2,1)S(1)} fusion(f32[2048,1280]{1,0:T(8,128)} %fusion.45, bf16[2048,2560]{1,0:T(8,128)(2,1)} %all-gather.17.cloned.1.call-done, bf16[2,2560,1280]{2,1,0:T(8,128)(2,1)} %param.26), kind=kOutput, calls=%fused_computation.47 | convolution fusion | flops 13437501440 | bytes 32768000 | tf_op jit(solution)/shard_map/dot_general | solution.py:64
  398.5 18.7 %convolution_convert_fusion.3 = bf16[2048,2560]{1,0:T(8,128)(2,1)} fusion(bf16[2048,1280]{1,0:T(8,128)(2,1)S(1)} %multiply_convert_fusion.1, bf16[2,1280,2560]{2,1,0:T(8,128)(2,1)} %param.27), kind=kOutput, calls=%fused_computation.44 | convolution fusion | flops 13427015680 | bytes 22282240 | tf_op jit(solution)/shard_map/dot_general | solution.py:64
  417.3 60.3 %reduce-scatter.7.cloned.1.call-done = bf16[256,2560]{1,0:T(8,128)(2,1)} async-done(((bf16[2048,2560]{1,0:T(8,128)(2,1)}), bf16[256,2560]{1,0:T(8,128)(2,1)}) %reduce-scatter.7.cloned.1.call-update) | async-done | bytes 1310736 | tf_op jit(solution)/shard_map/reduce_scatter | solution.py:106
  481.9 6.6 constant_dynamic-slice_fusion.3
  488.4 48.9 %all-gather.19.cloned.1.call-done = bf16[2048,2560]{1,0:T(8,128)(2,1)} async-done(((bf16[256,2560]{1,0:T(8,128)(2,1)}), bf16[2048,2560]{1,0:T(8,128)(2,1)}) %all-gather.19.cloned.1.call-update) | async-done | bytes 10485776 | tf_op jit(solution)/shard_map/all_gather | solution.py:89
  537.3 6.2 fusion.74
  543.5 5.6 fusion.76
  560.5 7.8 convolution_convert_fusion.5
  570.6 29.6 %all-gather.21.cloned.1.call-done = bf16[8192,1,256]{0,2,1:T(8,128)(2,1)} async-done(((bf16[2048,1,256]{0,2,1:T(8,128)(2,1)}), bf16[8192,1,256]{0,2,1:T(8,128)(2,1)}) %all-gather.21.cloned.1.call-update) | async-done | bytes 4194320 | tf_op jit(solution)/shard_map/all_gather | solution.py:97
  600.2 6.4 copy.51
  606.6 41.1 %all-gather.27.cloned.1.call-done = bf16[8192,256]{1,0:T(8,128)(2,1)} async-done(((bf16[2048,256]{1,0:T(8,128)(2,1)}), bf16[8192,256]{1,0:T(8,128)(2,1)}) %all-gather.27.cloned.1.call-update) | async-done | bytes 4194320 | tf_op jit(solution)/shard_map/all_gather | solution.py:98
  647.7 74.9 %while.29 = (s32[]{:T(128)}, bf16[8,256,1,1,256]{4,1,3,2,0:T(8,128)(2,1)S(1)}, s32[8]{0:T(128)S(1)}, s32[]{:T(128)}, s32[8192]{0:T(1024)S(1)}, /*index=5*/s32[8,...) while((s32[]{:T(128)}, ...), condition=%wide.region_12.13_spmd, body=%wide.region_9.12_spmd.sunk | while | flops 2170625792 | bytes 50702588 | solution.py:59
  722.6 6.8 convolution_convert_fusion.2
  729.6 61.2 %reduce-scatter.9.cloned.1.call-done = bf16[256,2560]{1,0:T(8,128)(2,1)} async-done(((bf16[2048,2560]{1,0:T(8,128)(2,1)}), bf16[256,2560]{1,0:T(8,128)(2,1)}) %reduce-scatter.9.cloned.1.call-update) | async-done | bytes 1310736 | tf_op jit(solution)/shard_map/reduce_scatter | solution.py:101
  794.7 55.5 %all-gather.23.cloned.1.call-done = bf16[2048,2560]{1,0:T(8,128)(2,1)} async-done(((bf16[256,2560]{1,0:T(8,128)(2,1)}), bf16[2048,2560]{1,0:T(8,128)(2,1)}) %all-gather.23.cloned.1.call-update) | async-done | bytes 10485776 | tf_op jit(solution)/shard_map/all_gather | solution.py:103
  850.1 19.3 %fusion.41 = f32[2048,1280]{1,0:T(8,128)} fusion(bf16[2048,2560]{1,0:T(8,128)(2,1)} %all-gather.23.cloned.1.call-done, bf16[2,2560,1280]{2,1,0:T(8,128)(2,1)} %param.25), kind=kOutput, calls=%fused_computation.50 | convolution fusion | flops 13421772800 | bytes 27525120 | tf_op jit(solution)/shard_map/dot_general | solution.py:64
  869.5 19.7 %multiply_convert_fusion = bf16[2048,1280]{1,0:T(8,128)(2,1)S(1)} fusion(f32[2048,1280]{1,0:T(8,128)} %fusion.41, bf16[2048,2560]{1,0:T(8,128)(2,1)} %all-gather.23.cloned.1.call-done, bf16[2,2560,1280]{2,1,0:T(8,128)(2,1)} %param.26), kind=kOutput, calls=%fused_computation.46 | convolution fusion | flops 13437501440 | bytes 32768000 | tf_op jit(solution)/shard_map/dot_general | solution.py:64
  889.2 18.7 %convolution_convert_fusion.1 = bf16[2048,2560]{1,0:T(8,128)(2,1)} fusion(bf16[2048,1280]{1,0:T(8,128)(2,1)S(1)} %multiply_convert_fusion, bf16[2,1280,2560]{2,1,0:T(8,128)(2,1)} %param.27), kind=kOutput, calls=%fused_computation.42 | convolution fusion | flops 13427015680 | bytes 22282240 | tf_op jit(solution)/shard_map/dot_general | solution.py:64
  907.9 60.4 %reduce-scatter.11.cloned.1.call-done = bf16[256,2560]{1,0:T(8,128)(2,1)} async-done(((bf16[2048,2560]{1,0:T(8,128)(2,1)}), bf16[256,2560]{1,0:T(8,128)(2,1)}) %reduce-scatter.11.cloned.1.call-update) | async-done | bytes 1310736 | tf_op jit(solution)/shard_map/reduce_scatter | solution.py:106
  (234 shorter events, 170.0 us)
Async XLA Ops:
  6.5 5.4 copy-start.8
  6.5 63.3 %all-gather.13.cloned.1.call-start = ((), (), s32[]{:S(2)}) async-start(), calls=%async_computation.4 | async-start | bytes 11796480 | tf_op jit(solution)/shard_map/all_gather | solution.py:89
  11.9 130.0 %all-gather.15.cloned.1.call-start = ((), (), s32[]{:S(2)}) async-start(), calls=%async_computation.5 | async-start | bytes 5242880 | tf_op jit(solution)/shard_map/all_gather | solution.py:97
  87.5 92.9 %all-gather.25.cloned.1.call-start = ((), (), s32[]{:S(2)}) async-start(), calls=%async_computation.14 | async-start | bytes 5242880 | tf_op jit(solution)/shard_map/all_gather | solution.py:98
  99.7 8.0 copy-start.9
  107.6 192.6 %reduce-scatter.5.cloned.1.call-start = ((), (), s32[]{:S(2)}) async-start(), calls=%async_computation.6 | async-start | bytes 11796480 | tf_op jit(solution)/shard_map/reduce_scatter | solution.py:101
  180.4 51.7 %copy-start.4 = (bf16[2,1,256,2560]{3,2,1,0:T(8,128)(2,1)S(1)}, bf16[2,1,256,2560]{3,2,1,0:T(8,128)(2,1)}, u32[]{:S(2)}) copy-start(bf16[2,1,256,2560]{3,2,1,0:T(8,128)(2,1)} %param.23) | copy-start | bytes 7864324
  238.9 0.7 copy-start.7
  238.9 61.3 %copy-start = (bf16[256,2560]{1,0:T(8,128)(2,1)S(1)}, bf16[256,2560]{1,0:T(8,128)(2,1)}, u32[]{:S(2)}) copy-start(bf16[256,2560]{1,0:T(8,128)(2,1)} %param.16) | copy-start | bytes 3932164
  239.0 120.7 %all-gather.17.cloned.1.call-start = ((), (), s32[]{:S(2)}) async-start(), calls=%async_computation.7 | async-start | bytes 11796480 | tf_op jit(solution)/shard_map/all_gather | solution.py:103
  300.2 1.9 copy-start.2
  303.9 173.7 %reduce-scatter.7.cloned.1.call-start = ((), (), s32[]{:S(2)}) async-start(), calls=%async_computation.8 | async-start | bytes 11796480 | tf_op jit(solution)/shard_map/reduce_scatter | solution.py:106
  417.3 120.0 %all-gather.19.cloned.1.call-start = ((), (), s32[]{:S(2)}) async-start(), calls=%async_computation.9 | async-start | bytes 11796480 | tf_op jit(solution)/shard_map/all_gather | solution.py:89
  481.6 118.6 %all-gather.21.cloned.1.call-start = ((), (), s32[]{:S(2)}) async-start(), calls=%async_computation.10 | async-start | bytes 5242880 | tf_op jit(solution)/shard_map/all_gather | solution.py:97
  537.3 6.2 copy-start.3
  555.1 92.7 %all-gather.27.cloned.1.call-start = ((), (), s32[]{:S(2)}) async-start(), calls=%async_computation.15 | async-start | bytes 5242880 | tf_op jit(solution)/shard_map/all_gather | solution.py:98
  568.4 222.4 %reduce-scatter.9.cloned.1.call-start = ((), (), s32[]{:S(2)}) async-start(), calls=%async_computation.11 | async-start | bytes 11796480 | tf_op jit(solution)/shard_map/reduce_scatter | solution.py:101
  570.6 77.1 %copy-start.5 = (bf16[8,256,1,1,256]{4,1,3,2,0:T(8,128)(2,1)S(1)}, bf16[8,256,1,1,256]{4,1,3,2,0:T(8,128)(2,1)}, u32[]{:S(2)}) copy-start(bf16[8,256,1,1,256]{4,1,3,2,0:T(8,128)(2,1)} %custom-call.1) | copy-start | bytes 3145732
  653.4 2.2 copy-start.10
  662.7 2.2 copy-start.10
  672.1 2.2 copy-start.10
  681.5 2.2 copy-start.10
  690.8 2.2 copy-start.10
  700.2 2.2 copy-start.10
  709.6 2.2 copy-start.10
  718.9 2.2 copy-start.10
  729.5 63.2 %copy-start.6 = (f32[2560]{0:T(1024)S(1)}, f32[2560]{0:T(1024)}, u32[]{:S(2)}) copy-start(f32[2560]{0:T(1024)} %get-tuple-element.422) | copy-start | bytes 30724
  729.5 120.6 %all-gather.23.cloned.1.call-start = ((), (), s32[]{:S(2)}) async-start(), calls=%async_computation.12 | async-start | bytes 11796480 | tf_op jit(solution)/shard_map/all_gather | solution.py:103
  790.8 1.9 copy-start.1
  794.4 173.8 %reduce-scatter.11.cloned.1.call-start = ((), (), s32[]{:S(2)}) async-start(), calls=%async_computation.13 | async-start | bytes 11796480 | tf_op jit(solution)/shard_map/reduce_scatter | solution.py:106
Sparse Core Ops, SparseCore 0:
  12.0 57.8 all-gather.12
  87.6 45.1 all-gather.14
  134.4 45.9 all-gather.24
  239.1 61.1 reduce-scatter.4
  304.1 55.5 all-gather.16
  417.4 60.2 reduce-scatter.6
  481.7 55.5 all-gather.18
  555.2 44.9 all-gather.20
  601.8 45.9 all-gather.26
  729.7 61.1 reduce-scatter.8
  794.6 55.5 all-gather.22
  908.0 60.2 reduce-scatter.10
where the time goes:
time: 989 us; the launch traced here: 978 us
  waiting for transfers between devices  534 us (54%)
  matrix products  248 us (25%)
  local copies, waits for them, and re-layouts  67 us (7%)
  blocking collectives  56 us (6%)
  other arithmetic  46.8 us (5%)
  between operations  14 us (1%)
  loops' own time  10.8 us (1%)
    dot_general x14, matrix products, matmul(): return jnp.dot(rows_in, weight, preferred_element_type=jnp.float32)  168 us
    reduce_scatter x2, waiting for transfers between devices, local_fn(): attn_out = lax.psum_scatter(part_sum, 'tp', scatter_dimension=0, tiled=True)  121 us
    reduce_scatter x2, waiting for transfers between devices, local_fn(): mlp_out = lax.psum_scatter(part_sum, 'tp', scatter_dimension=0, tiled=True)  121 us
    all_gather x2, waiting for transfers between devices, local_fn(): normed = lax.all_gather(rms_norm(hidden, g_mlp[layer]), 'tp', tiled=True)  111 us
    all_gather x2, waiting for transfers between devices, local_fn(): lax.all_gather(v.reshape(shard_rows, kv_loc, head_dim), 'sp', tiled=True)  79.6 us
    all_gather x2, waiting for transfers between devices, local_fn(): normed = lax.all_gather(rms_norm(x, g_attn[layer]), 'tp', tiled=True)  71 us
    dot_general x16, matrix products, one_block(): jnp.einsum('qgrd,kgd->qgrk', q_blk, k_blk, preferred_element_type=jnp.flo...  54.9 us
    all_gather x1, blocking collectives, local_fn(): seg_all = lax.all_gather(segment_ids, ('sp', 'tp'), tiled=True)  32.4 us
  transfers between devices with their start and end apart: 12, of which 11 were waited for; matrix products, arithmetic and copies ran while one was open for 6% of the time, Pallas kernels for 0%

commit v1 on v0

v1 whole, which is shorter than its diff:
```python
import functools
import math

import jax
import jax.numpy as jnp
from jax import lax
from jax.experimental import pallas as pl
from jax.experimental.pallas import tpu as pltpu
from jax.sharding import PartitionSpec as P

EPS = 1e-6
ROPE_BASE = 10000.0
WINDOW = 1024
CHIPS = 4
MESH = pl.DeviceIdType.MESH
BF16 = jnp.bfloat16
F32 = jnp.float32
VMEM_LIMIT = 66_000_000
Q_BLOCK = 512
K_BLOCK = 512


def _place():
    t = lax.axis_index("tp")
    c = lax.rem(t, 2)
    x = t // 2
    right = lax.rem(x + 1, CHIPS) * 2 + c
    left = lax.rem(x + CHIPS - 1, CHIPS) * 2 + c
    sib = x * 2 + 1 - c
    return x, c, right, left, sib


def _copy(src, dst, sems, index, axis, dev):
    send, recv = sems
    return pltpu.make_async_remote_copy(
        src_ref=src, dst_ref=dst, send_sem=send.at[index], recv_sem=recv.at[index],
        device_id={axis: dev}, device_id_type=MESH)


def _barrier(peers):
    bar = pltpu.get_barrier_semaphore()
    for axis, dev in peers:
        pl.semaphore_signal(bar, inc=1, device_id={axis: dev}, device_id_type=MESH)
    pl.semaphore_wait(bar, len(peers))


def _piece_rows(x, c, rows, k, j):
    half = rows // 2
    core = c if j < 2 else 1 - c
    even = j % 2 == 0
    if k == 0:
        chip, h = x, j % 2
    elif k == 1:
        chip, h = (x + CHIPS - 1, 0) if even else (x + 1, 1)
    elif k == 2:
        chip, h = (x + CHIPS - 1, 1) if even else (x + 1, 0)
    else:
        chip, h = x + 2, j % 2
    return lax.rem(chip, CHIPS) * (2 * rows) + core * rows + h * half


def _gather_copies(buf, sems, rows, right, left, sib):
    half = rows // 2
    a, b = pl.ds(0, half), pl.ds(half, half)
    ring = [
        _copy(buf.at[0, a], buf.at[1, a], sems, 0, "tp", right),
        _copy(buf.at[0, b], buf.at[1, b], sems, 1, "tp", left),
        _copy(buf.at[0, b], buf.at[2, a], sems, 2, "tp", right),
        _copy(buf.at[0, a], buf.at[2, b], sems, 3, "tp", left),
        _copy(buf.at[1, a], buf.at[3, a], sems, 4, "tp", right),
        _copy(buf.at[1, b], buf.at[3, b], sems, 5, "tp", left),
    ]
    relay = [_copy(buf.at[k, pl.ds(0, rows)], buf.at[k, pl.ds(rows, rows)], sems, 6 + k, "tp", sib) for k in range(4)]
    return ring, relay


def _gather_begin(ring, relay):
    for i in (0, 1):
        ring[i].start()
    relay[0].start()
    for i in (2, 3):
        ring[i].start()


def _gather_arrive(ring, relay, k):
    if k == 1:
        ring[0].wait_recv()
        ring[4].start()
        ring[1].wait_recv()
        ring[5].start()
    elif k >= 2:
        ring[2 * k - 2].wait_recv()
        ring[2 * k - 1].wait_recv()
    if k >= 1:
        relay[k].start()
    relay[k].wait_recv()


def _gather_end(ring, relay):
    for copy in ring + relay:
        copy.wait_send()


def _norm_into(dst, x_ref, g_ref):
    rows = x_ref.shape[0]
    gain = g_ref[...].astype(F32)
    chunk = 16

    def body(i, carry):
        rs = pl.ds(pl.multiple_of(i * chunk, chunk), chunk)
        wide = x_ref[rs, :].astype(F32)
        inv = lax.rsqrt(jnp.mean(wide * wide, axis=-1, keepdims=True) + EPS)
        dst[0, rs, :] = (wide * inv * gain).astype(BF16)
        return carry

    lax.fori_loop(0, rows // chunk, body, 0)


def _add_rows(rows, body):
    chunk = 16

    def step(i, carry):
        body(pl.ds(pl.multiple_of(i * chunk, chunk), chunk))
        return carry

    lax.fori_loop(0, rows // chunk, step, 0)


class _Scatter:
    def __init__(self, part, from_sib, direct, chain, last, sems, rows, right, left, sib):
        half = rows // 2
        a, b = pl.ds(0, half), pl.ds(half, half)
        self.rows, self.part, self.from_sib = rows, part, from_sib
        self.direct, self.chain, self.last = direct, chain, last
        self.swap = [_copy(part.at[k, pl.ds(rows, rows)], from_sib.at[k], sems, k, "tp", sib) for k in range(4)]
        self.d = [_copy(part.at[2, b], direct.at[a], sems, 4, "tp", right), _copy(part.at[2, a], direct.at[b], sems, 5, "tp", left)]
        self.c = [_copy(part.at[3, b], chain.at[b], sems, 6, "tp", right), _copy(part.at[3, a], chain.at[a], sems, 7, "tp", left)]
        self.l = [_copy(part.at[1, b], last.at[b], sems, 8, "tp", right), _copy(part.at[1, a], last.at[a], sems, 9, "tp", left)]

    def _fold(self, k, extra=None):
        part, from_sib = self.part, self.from_sib

        def body(rs):
            total = part[k, rs, :].astype(F32) + from_sib[k, rs, :].astype(F32)
            if extra is not None:
                total = total + extra[rs, :].astype(F32)
            part[k, rs, :] = total.astype(BF16)

        _add_rows(self.rows, body)

    def send_direct(self):
        self.swap[2].wait_recv()
        self._fold(2)
        for copy in self.d:
            copy.start()

    def send_chain(self):
        self.swap[3].wait_recv()
        self._fold(3)
        for copy in self.c:
            copy.start()

    def forward_chain(self):
        self.swap[1].wait_recv()
        for copy in self.c:
            copy.wait_recv()
        self._fold(1, self.chain)
        for copy in self.l:
            copy.start()

    def finish(self, o_ref, x_ref):
        self.swap[0].wait_recv()
        for copy in self.d + self.l:
            copy.wait_recv()
        part, from_sib, direct, last = self.part, self.from_sib, self.direct, self.last

        def body(rs):
            total = part[0, rs, :].astype(F32) + from_sib[0, rs, :].astype(F32)
            total = total + direct[rs, :].astype(F32) + last[rs, :].astype(F32)
            o_ref[rs, :] = (x_ref[rs, :].astype(F32) + total.astype(BF16).astype(F32)).astype(BF16)

        _add_rows(self.rows, body)
        for copy in self.swap + self.d + self.c + self.l:
            copy.wait_send()


def _scatter_scratch(rows, model):
    return [
        pltpu.VMEM((4, 2 * rows, model), BF16),
        pltpu.VMEM((4, rows, model), BF16),
        pltpu.VMEM((rows, model), BF16),
        pltpu.VMEM((rows, model), BF16),
        pltpu.VMEM((rows, model), BF16),
        pltpu.SemaphoreType.DMA((10,)),
        pltpu.SemaphoreType.DMA((10,)),
    ]


def _params(collective_id):
    return pltpu.CompilerParams(collective_id=collective_id, has_side_effects=True, vmem_limit_bytes=VMEM_LIMIT)


def _mlp_kernel(layer, x_ref, g_ref, wg_hbm, wu_hbm, wd_hbm, o_ref, buf, wg, wu, wd, act, part, from_sib, direct, chain, last,
                s_send, s_recv, g_send, g_recv, w_sem):
    rows, model = x_ref.shape
    cols = wg.shape[1]
    x, c, right, left, sib = _place()
    loads = [pltpu.make_async_copy(src.at[layer], dst, w_sem.at[i]) for i, (src, dst) in enumerate(((wg_hbm, wg), (wu_hbm, wu), (wd_hbm, wd)))]
    for load in loads:
        load.start()
    _norm_into(buf, x_ref, g_ref)
    _barrier((("tp", left), ("tp", right), ("tp", sib)))
    ring, relay = _gather_copies(buf, (g_send, g_recv), rows, right, left, sib)
    _gather_begin(ring, relay)
    scatter = _Scatter(part, from_sib, direct, chain, last, (s_send, s_recv), rows, right, left, sib)
    nt = 256

    def step(k, carry):
        for kk in range(4):
            @pl.when(k == kk)
            def _():
                _gather_arrive(ring, relay, kk)
                if kk == 0:
                    loads[0].wait()
                    loads[1].wait()

        def up(n, inner):
            cs = pl.ds(pl.multiple_of(n * nt, nt), nt)
            gate = jnp.dot(buf[k], wg[:, cs], preferred_element_type=F32)
            lin = jnp.dot(buf[k], wu[:, cs], preferred_element_type=F32)
            act[:, cs] = (jax.nn.silu(gate) * lin).astype(BF16)
            return inner

        lax.fori_loop(0, cols // nt, up, 0)

        @pl.when(k == 0)
        def _():
            loads[2].wait()

        def down(n, inner):
            cs = pl.ds(pl.multiple_of(n * nt, nt), nt)
            part[k, :, cs] = jnp.dot(act[...], wd[:, cs], preferred_element_type=F32).astype(BF16)
            return inner

        lax.fori_loop(0, model // nt, down, 0)
        for kk in range(4):
            @pl.when(k == kk)
            def _():
                scatter.swap[kk].start()
                if kk == 2:
                    scatter.send_direct()
                if kk == 3:
                    scatter.send_chain()
        return carry

    lax.fori_loop(0, 4, step, 0)
    scatter.forward_chain()
    scatter.finish(o_ref, x_ref)
    _gather_end(ring, relay)


def _mlp(layer, x, gain, w_gate, w_up, w_down):
    rows, model = x.shape
    cols = w_gate.shape[2]
    vmem, hbm = pl.BlockSpec(memory_space=pltpu.VMEM), pl.BlockSpec(memory_space=pl.ANY)
    return pl.pallas_call(
        functools.partial(_mlp_kernel, layer),
        name=f"mlp_{layer}",
        out_shape=jax.ShapeDtypeStruct((rows, model), BF16),
        in_specs=[vmem, vmem, hbm, hbm, hbm],
        out_specs=vmem,
        scratch_shapes=[
            pltpu.VMEM((4, 2 * rows, model), BF16),
            pltpu.VMEM((model, cols), BF16),
            pltpu.VMEM((model, cols), BF16),
            pltpu.VMEM((cols, model), BF16),
            pltpu.VMEM((2 * rows, cols), BF16),
            *_scatter_scratch(rows, model),
            pltpu.SemaphoreType.DMA((10,)),
            pltpu.SemaphoreType.DMA((10,)),
            pltpu.SemaphoreType.DMA((3,)),
        ],
        compiler_params=_params(layer),
    )(x, gain, w_gate, w_up, w_down)


def _out_kernel(layer, m_ref, x_ref, wo_hbm, o_ref, wo, lhs, part, from_sib, direct, chain, last, s_send, s_recv, w_sem):
    rows, model = x_ref.shape
    half = rows // 2
    x, c, right, left, sib = _place()
    load = pltpu.make_async_copy(wo_hbm.at[layer], wo, w_sem.at[0])
    load.start()
    _barrier((("tp", left), ("tp", right), ("tp", sib)))
    scatter = _Scatter(part, from_sib, direct, chain, last, (s_send, s_recv), rows, right, left, sib)
    load.wait()
    nt = 512
    for k in (2, 3, 1, 0):
        for j in range(4):
            start = pl.multiple_of(_piece_rows(x, c, rows, k, j), half)
            lhs[pl.ds(j * half, half), :] = m_ref[pl.ds(start, half), :]

        def down(n, inner):
            cs = pl.ds(pl.multiple_of(n * nt, nt), nt)
            part[k, :, cs] = jnp.dot(lhs[...], wo[:, cs], preferred_element_type=F32).astype(BF16)
            return inner

        lax.fori_loop(0, model // nt, down, 0)
        scatter.swap[k].start()
        if k == 2:
            scatter.send_direct()
        if k == 3:
            scatter.send_chain()
    scatter.forward_chain()
    scatter.finish(o_ref, x_ref)


def _out_proj(layer, mixed, x, w_o):
    rows, model = x.shape
    head_dim = mixed.shape[1]
    vmem, hbm = pl.BlockSpec(memory_space=pltpu.VMEM), pl.BlockSpec(memory_space=pl.ANY)
    return pl.pallas_call(
        functools.partial(_out_kernel, layer),
        name=f"out_{layer}",
        out_shape=jax.ShapeDtypeStruct((rows, model), BF16),
        in_specs=[vmem, vmem, hbm],
        out_specs=vmem,
        scratch_shapes=[
            pltpu.VMEM((head_dim, model), BF16),
            pltpu.VMEM((2 * rows, head_dim), BF16),
            *_scatter_scratch(rows, model),
            pltpu.SemaphoreType.DMA((1,)),
        ],
        compiler_params=_params(2 + layer),
    )(mixed, x, w_o)


def _qkv_kernel(layer, gather_tab, windowed, shards, x_ref, g_ref, tab_in, wq_hbm, wkv_hbm, q_out, kv_out, *rest):
    if gather_tab:
        tab_out, rest = rest[0], rest[1:]
    buf, tab, wq, wkv, qs, kv, g_send, g_recv, t_send, t_recv, y_send, y_recv, p_send, p_recv, l_sem, q_sem, w_sem = rest
    rows, model = x_ref.shape
    half, step_rows = rows // 2, 2 * rows
    shard = 4 * step_rows
    hd = wq.shape[1]
    x, c, right, left, sib = _place()
    y = lax.axis_index("sp")
    up, down = lax.rem(y + 1, shards), lax.rem(y + shards - 1, shards)
    loads = [pltpu.make_async_copy(wq_hbm.at[layer], wq, w_sem.at[0]), pltpu.make_async_copy(wkv_hbm.at[layer], wkv, w_sem.at[1])]
    for load in loads:
        load.start()
    if not gather_tab:
        tab_load = pltpu.make_async_copy(tab_in, tab, w_sem.at[2])
        tab_load.start()
    else:
        tab_load = pltpu.make_async_copy(tab_in, tab.at[0, pl.ds(0, rows)], w_sem.at[2])
        tab_load.start()
    _norm_into(buf, x_ref, g_ref)
    tab_load.wait()
    _barrier((("tp", left), ("tp", right), ("tp", sib), ("sp", up), ("sp", down)))
    ring, relay = _gather_copies(buf, (g_send, g_recv), rows, right, left, sib)
    if gather_tab:
        t_ring, t_relay = _gather_copies(tab, (t_send, t_recv), rows, right, left, sib)
        for i in (0, 1):
            t_ring[i].start()
            ring[i].start()
        t_relay[0].start()
        relay[0].start()
        for i in (2, 3):
            t_ring[i].start()
            ring[i].start()
    else:
        _gather_begin(ring, relay)

    if windowed:
        bases = (shard, 0)
    else:
        bases = tuple(lax.rem(y + d, shards) * shard for d in (0, shards - 1, 1, 2))

    def y_copies(k):
        whole, a, b = pl.ds(k * step_rows, step_rows), pl.ds(k * step_rows, rows), pl.ds(k * step_rows + rows, rows)
        sems = (y_send, y_recv)
        first = [_copy(kv.at[0, whole], kv.at[1, whole], sems, 4 * k, "sp", up)]
        second = []
        if not windowed:
            first.append(_copy(kv.at[0, whole], kv.at[2, whole], sems, 4 * k + 1, "sp", down))
            second.append(_copy(kv.at[1, a], kv.at[3, a], sems, 4 * k + 2, "sp", up))
            second.append(_copy(kv.at[2, b], kv.at[3, b], sems, 4 * k + 3, "sp", down))
        return first, second

    def place(s, k):
        for j in range(4):
            src = kv.at[s, pl.ds(k * step_rows + j * half, half)]
            start = pl.multiple_of(bases[s] + _piece_rows(x, c, rows, k, j), half)
            dst = kv_out.at[c, pl.ds(start, half)]
            pltpu.make_async_copy(src, dst, l_sem.at[s]).start()
            _copy(src, dst, (p_send, p_recv), s, "tp", sib).start()

    def forward(k):
        first, second = y_copies(k)
        for copy in first:
            copy.wait_recv()
        for copy in second:
            copy.start()
        place(1, k)
        if not windowed:
            place(2, k)

    def opposite(k):
        first, second = y_copies(k)
        for copy in second:
            copy.wait_recv()
        if second:
            place(3, k)

    def step(k, carry):
        for kk in range(4):
            @pl.when(k == kk)
            def _():
                if kk == 0:
                    loads[0].wait()
                    loads[1].wait()
                if gather_tab:
                    _gather_arrive(t_ring, t_relay, kk)
                _gather_arrive(ring, relay, kk)

        cos, sin = tab[k, :, :hd // 2], tab[k, :, hd // 2:]

        def rotate(t):
            lower, upper = t[:, :hd // 2], t[:, hd // 2:]
            return jnp.concatenate([lower * cos - upper * sin, upper * cos + lower * sin], axis=-1).astype(BF16)

        q = jnp.dot(buf[k], wq[...], preferred_element_type=F32).astype(BF16).astype(F32)
        rs = pl.ds(pl.multiple_of(k * step_rows, step_rows), step_rows)
        qs[rs, :] = rotate(q)
        t = jnp.dot(buf[k], wkv[...], preferred_element_type=F32).astype(BF16)

        @pl.when(c == 0)
        def _():
            kv[0, rs, :] = rotate(t.astype(F32))

        @pl.when(c == 1)
        def _():
            kv[0, rs, :] = t

        for kk in range(4):
            @pl.when(k == kk)
            def _():
                for copy in y_copies(kk)[0]:
                    copy.start()
                for j in range(4):
                    start = pl.multiple_of(_piece_rows(x, c, rows, kk, j), half)
                    pltpu.make_async_copy(qs.at[pl.ds(kk * step_rows + j * half, half)], q_out.at[pl.ds(start, half)], q_sem.at[0]).start()
                place(0, kk)
                if kk >= 1:
                    forward(kk - 1)
                if kk >= 2:
                    opposite(kk - 2)
        return carry

    lax.fori_loop(0, 4, step, 0)
    forward(3)
    opposite(2)
    opposite(3)
    if gather_tab:
        store = pltpu.make_async_copy(tab, tab_out, w_sem.at[3])
        store.start()
        store.wait()
        _gather_end(t_ring, t_relay)
    pltpu.make_async_copy(qs, q_out, q_sem.at[0]).wait()
    for s, base in enumerate(bases):
        span = pl.ds(pl.multiple_of(base, shard), shard)
        pltpu.make_async_copy(kv.at[s], kv_out.at[c, span], l_sem.at[s]).wait()
        swap = _copy(kv.at[s], kv_out.at[c, span], (p_send, p_recv), s, "tp", sib)
        swap.wait_send()
        swap.wait_recv()
    for k in range(4):
        first, second = y_copies(k)
        for copy in first + second:
            copy.wait_send()
    _gather_end(ring, relay)


def _qkv(layer, windowed, shards, x, gain, tab, w_q, w_kv):
    rows, model = x.shape
    hd = w_q.shape[2]
    gather_tab = tab.ndim == 2
    shard = 8 * rows
    held = 2 if windowed else shards
    vmem, hbm = pl.BlockSpec(memory_space=pltpu.VMEM), pl.BlockSpec(memory_space=pl.ANY)
    tab_shape = (4, 2 * rows, hd)
    out_shape = [jax.ShapeDtypeStruct((shard, hd), BF16), jax.ShapeDtypeStruct((2, held * shard, hd), BF16)]
    if gather_tab:
        out_shape.append(jax.ShapeDtypeStruct(tab_shape, F32))
    return pl.pallas_call(
        functools.partial(_qkv_kernel, layer, gather_tab, windowed, shards),
        name=f"qkv_{layer}",
        out_shape=out_shape,
        in_specs=[vmem, vmem, hbm, hbm, hbm],
        out_specs=[hbm] * len(out_shape),
        scratch_shapes=[
            pltpu.VMEM((4, 2 * rows, model), BF16),
            pltpu.VMEM(tab_shape, F32),
            pltpu.VMEM((model, hd), BF16),
            pltpu.VMEM((model, hd), BF16),
            pltpu.VMEM((shard, hd), BF16),
            pltpu.VMEM((held, shard, hd), BF16),
            pltpu.SemaphoreType.DMA((10,)),
            pltpu.SemaphoreType.DMA((10,)),
            pltpu.SemaphoreType.DMA((10,)),
            pltpu.SemaphoreType.DMA((10,)),
            pltpu.SemaphoreType.DMA((16,)),
            pltpu.SemaphoreType.DMA((16,)),
            pltpu.SemaphoreType.DMA((4,)),
            pltpu.SemaphoreType.DMA((4,)),
            pltpu.SemaphoreType.DMA((4,)),
            pltpu.SemaphoreType.DMA((1,)),
            pltpu.SemaphoreType.DMA((4,)),
        ],
        compiler_params=_params(4 + layer),
    )(x, gain, tab, w_q, w_kv)


def _attend_kernel(scale, bounds, q_ref, lo_ref, kv_ref, o_ref, m_sc, l_sc, acc_sc):
    i = pl.program_id(0)
    rows, hd = q_ref.shape
    m_sc[...] = jnp.full(m_sc.shape, -1e30, F32)
    l_sc[...] = jnp.zeros(l_sc.shape, F32)
    acc_sc[...] = jnp.zeros(acc_sc.shape, F32)
    first = bounds[4, i]

    def block(masked, b, carry):
        start = pl.multiple_of(b * K_BLOCK, K_BLOCK)
        k = kv_ref[0, pl.ds(start, K_BLOCK), :]
        v = kv_ref[1, pl.ds(start, K_BLOCK), :]
        s = lax.dot_general(q_ref[...], k, (((1,), (1,)), ((), ())), preferred_element_type=F32)
        if masked:
            j = start + lax.broadcasted_iota(jnp.int32, (rows, K_BLOCK), 1)
            r = first + lax.broadcasted_iota(jnp.int32, (rows, K_BLOCK), 0)
            s = jnp.where((j <= r) & (j >= lo_ref[...]), s, -1e30)
        m_old = m_sc[...]
        m_new = jnp.maximum(m_old, jnp.max(s, axis=1, keepdims=True))
        p = jnp.exp2((s - m_new) * scale)
        alpha = jnp.exp2((m_old - m_new) * scale)
        m_sc[...] = m_new
        l_sc[...] = l_sc[...] * alpha + jnp.sum(p, axis=1, keepdims=True)
        acc_sc[...] = acc_sc[...] * alpha + jnp.dot(p.astype(BF16), v, preferred_element_type=F32)
        return carry

    lax.fori_loop(bounds[0, i], bounds[1, i], functools.partial(block, True), 0)
    lax.fori_loop(bounds[1, i], bounds[2, i], functools.partial(block, False), 0)
    lax.fori_loop(bounds[2, i], bounds[3, i], functools.partial(block, True), 0)
    o_ref[...] = (acc_sc[...] / l_sc[...]).astype(BF16)


def _attend(q, kv, row_lo, first_row):
    total, hd = q.shape
    blocks = total // Q_BLOCK
    lo2 = row_lo.reshape(blocks, Q_BLOCK)
    first = first_row + jnp.arange(blocks, dtype=jnp.int32) * Q_BLOCK
    b_lo = lo2[:, 0] // K_BLOCK
    b_hi = (first + Q_BLOCK - 1) // K_BLOCK + 1
    b_a = jnp.clip((lo2[:, -1] + K_BLOCK - 1) // K_BLOCK, b_lo, b_hi)
    b_b = jnp.clip((first + 1) // K_BLOCK, b_a, b_hi)
    bounds = jnp.stack([b_lo, b_a, b_b, b_hi, first]).astype(jnp.int32)
    return pl.pallas_call(
        functools.partial(_attend_kernel, hd ** -0.5 * math.log2(math.e)),
        name="attend",
        out_shape=jax.ShapeDtypeStruct((total, hd), BF16),
        grid_spec=pltpu.PrefetchScalarGridSpec(
            num_scalar_prefetch=1,
            grid=(blocks,),
            in_specs=[
                pl.BlockSpec((Q_BLOCK, hd), lambda i, b: (i, 0)),
                pl.BlockSpec((Q_BLOCK, 1), lambda i, b: (i, 0)),
                pl.BlockSpec(memory_space=pltpu.VMEM),
            ],
            out_specs=pl.BlockSpec((Q_BLOCK, hd), lambda i, b: (i, 0)),
            scratch_shapes=[pltpu.VMEM((Q_BLOCK, 1), F32), pltpu.VMEM((Q_BLOCK, 1), F32), pltpu.VMEM((Q_BLOCK, hd), F32)],
        ),
        compiler_params=pltpu.CompilerParams(dimension_semantics=("arbitrary",), vmem_limit_bytes=VMEM_LIMIT),
    )(bounds, q, row_lo.reshape(total, 1), kv)


def solution(mesh):
    tp_size, shards = mesh.shape["tp"], mesh.shape["sp"]
    row_spec = P(("dp", "sp", "tp"), None)
    id_spec = P(("dp", "sp", "tp"))
    whole = P()
    in_specs = (row_spec, id_spec, id_spec, whole, P(None, None, "tp", None), whole, whole, P(None, "tp", None, None), whole, P(None, None, "tp"), P(None, None, "tp"), P(None, "tp", None))

    def local_fn(x, segment_ids, positions, g_attn, w_q, w_k, w_v, w_o, g_mlp, w_gate, w_up, w_down):
        sp_idx = lax.axis_index("sp")
        tp_idx = lax.axis_index("tp")
        layers, model, heads_loc, hd = w_q.shape
        rows = x.shape[0]
        shard = rows * tp_size
        kv_head = tp_idx * w_k.shape[2] // tp_size
        inv_freq = ROPE_BASE ** (-jnp.arange(hd // 2, dtype=F32) / (hd // 2))
        angles = positions.astype(F32)[:, None] * inv_freq[None, :]
        tab = jnp.concatenate([jnp.cos(angles), jnp.sin(angles)], axis=1)
        seg_all = lax.all_gather(segment_ids, ("sp", "tp"), tiled=True)
        second, third = jnp.sum(seg_all < 1), jnp.sum(seg_all < 2)
        token = sp_idx * shard + jnp.arange(shard, dtype=jnp.int32)
        seg_lo = jnp.where(token >= third, third, jnp.where(token >= second, second, 0)).astype(jnp.int32)
        pick_k = lax.dynamic_slice_in_dim(w_k, kv_head, 1, 2).reshape(layers, model, hd)
        pick_v = lax.dynamic_slice_in_dim(w_v, kv_head, 1, 2).reshape(layers, model, hd)
        w_kv = jnp.where(tp_idx % 2 == 0, pick_k, pick_v)
        w_q2 = w_q.reshape(layers, model, hd)
        w_o2 = w_o.reshape(layers, hd, model)
        for layer in range(layers):
            windowed = layer % 2 == 0
            got = _qkv(layer, windowed, shards, x, g_attn[layer:layer + 1], tab, w_q2, w_kv)
            q, kv = got[0], got[1]
            if len(got) == 3:
                tab = got[2]
            if windowed:
                shift = (sp_idx - 1) * shard
                row_lo = jnp.maximum(seg_lo, token - (WINDOW - 1)) - shift
            else:
                shift = 0
                row_lo = seg_lo
            mixed = _attend(q, kv, row_lo, sp_idx * shard - shift)
            hidden = _out_proj(layer, mixed, x, w_o2)
            x = _mlp(layer, hidden, g_mlp[layer:layer + 1], w_gate, w_up, w_down)
        return x

    return jax.shard_map(local_fn, mesh=mesh, in_specs=in_specs, out_specs=row_spec, check_vma=False)
```

time: 989 us -> 609 us (0.62)
  waiting for transfers between devices: 534 us -> 0 us
  Pallas kernels: 0 us -> 532 us
  matrix products: 248 us -> 0 us
  local copies, waits for them, and re-layouts: 67 us -> 18.5 us
  other arithmetic: 46.8 us -> 14.1 us
  blocking collectives: 56 us -> 33.5 us
  between operations: 14 us -> 0.14 us
  loops' own time: 10.8 us -> 0 us
    pallas_call x0 -> x8, Pallas kernels: none -> 532 us  [the longest x2 225 us: _mlp(): pl.pallas_call(functools.partial(_mlp_kernel, layer), name=f'mlp_{layer}'...]
    all_gather x8 -> x0, waiting for transfers between devices: 291 us -> none  [the longest x2 111 us: local_fn(): normed = lax.all_gather(rms_norm(hidden, g_mlp[layer]), 'tp', tiled=True)]
    dot_general x46 -> x0, matrix products: 248 us -> none  [the longest x14 168 us: matmul(): return jnp.dot(rows_in, weight, preferred_element_type=jnp.float32)]
    reduce_scatter x4 -> x0, waiting for transfers between devices: 242 us -> none  [the longest x2 121 us: local_fn(): attn_out = lax.psum_scatter(part_sum, 'tp', scatter_dimension=0, tiled=True)]
    all_gather x1 -> x0, blocking collectives: 23.6 us -> none  [local_fn(): pos_shard = lax.all_gather(positions, 'tp', tiled=True)]
    reduce_sum x20 -> x1, other arithmetic: 20.8 us -> 0.81 us  [local_fn(): second, third = (jnp.sum(seg_all < 1), jnp.sum(seg_all < 2))]
    slice x2, local copies, waits for them, and re-layouts: 18.7 us -> 1.25 us  [the longest x1 0.63 us: local_fn(): g_attn[layer:layer + 1]]
    dynamic_slice x45 -> x1, local copies, waits for them, and re-layouts: 27.4 us -> 13.6 us  [local_fn(): lax.dynamic_slice_in_dim(w_v, kv_head, 1, 2).reshape(layers, model, hd)]
  transfers between devices with their start and end apart: 12 -> 0, of which waited for: 11 -> 0; matrix products, arithmetic and copies ran while one was open for 6% -> 0% of each run, Pallas kernels for 0% -> 0%
where the time goes in v1:
time: 609 us; the launch traced here: 599 us
  Pallas kernels  532 us (87%)
  blocking collectives  33.5 us (6%)
  local copies, waits for them, and re-layouts  18.5 us (3%)
  other arithmetic  14.1 us (2%)
    pallas_call x2, Pallas kernels, _mlp(): pl.pallas_call(functools.partial(_mlp_kernel, layer), name=f'mlp_{layer}'...  225 us
    pallas_call x2, Pallas kernels, _qkv(): pl.pallas_call(functools.partial(_qkv_kernel, layer, gather_tab, windowed...  142 us
    pallas_call x2, Pallas kernels, _out_proj(): pl.pallas_call(functools.partial(_out_kernel, layer), name=f'out_{layer}'...  114 us
    pallas_call x2, Pallas kernels, _attend(): pl.pallas_call(functools.partial(_attend_kernel, hd ** (-0.5) * math.log2...  51.3 us
    all_gather x1, blocking collectives, local_fn(): seg_all = lax.all_gather(segment_ids, ('sp', 'tp'), tiled=True)  33.5 us
    dynamic_slice x1, local copies, waits for them, and re-layouts, local_fn(): lax.dynamic_slice_in_dim(w_v, kv_head, 1, 2).reshape(layers, model, hd)  13.6 us

profile of v1, /device:TPU:112, one launch (start us, length us, event | category | flops | bytes accessed | tf_op | source)
XLA Modules:
  0.0 598.7 jit_solution(13766895566318956004)
XLA Ops:
  0.0 13.6 %constant_dynamic-slice_fusion = (bf16[2,2560,1,256]{3,2,1,0:T(2,128)(2,1)}, bf16[2,2560,1,256]{3,2,1,0:T(2,128)(2,1)}) fusion(bf16[2,2560,4,256]{3,2,1,0:T(4,128)(2,1)} %param.18, s32[]{:T(128)S(6)} %select_n.198, bf16[2,2560,4,256]{3,2,1,0:T(4,128)(2,1)} %param.17), kind=kLoop, calls=%fused_computation.67 | loop fusion | bytes 10485764 | tf_op jit(solution)/shard_map/dynamic_slice | solution.py:606
  13.6 0.0 copy-start.3
  13.6 0.0 copy-start
  13.6 6.2 %fusion.wkv_hbm = bf16[2,2560,256]{2,1,0:T(8,128)(2,1)} fusion(bf16[2,2560,1,256]{3,2,1,0:T(2,128)(2,1)} %get-tuple-element.36, bf16[2,2560,1,256]{3,2,1,0:T(2,128)(2,1)} %get-tuple-element.37, pred[]{:T(512)S(6)} %eq.5), kind=kLoop, calls=%fused_computation.1 | loop fusion | flops 1310720 | bytes 7864321 | tf_op jit(solution)/shard_map/jit(_where)/select_n | solution.py:607
  19.8 0.0 copy-done.3
  19.8 0.0 copy-start.2
  19.8 0.5 multiply_cosine_fusion
  20.4 0.7 pad_maximum_fusion.tab_in
  21.1 0.0 copy-done
  21.1 0.6 fusion.14
  21.7 71.6 %qkv_0.1 = (bf16[2048,256]{1,0:T(8,128)(2,1)}, bf16[2,4096,256]{2,1,0:T(8,128)(2,1)}, f32[4,512,256]{2,1,0:T(8,128)}) custom-call(bf16[256,2560]{1,0:T(8,128)(2,1)} %x_ref.3, bf16[1,2560]{1,0:T(2,128)(2,1)} %get-tuple-element.26.g_ref, f32[256,256]{1,0:T(8,128)} %pad_maximum_fusion.tab_in, bf16[2,2560,256]{2,1,0:T(8,128)(2,1)} %bitcast.25, ...), custom_call_target="tpu_custom_call" | custom-call | tf_op jit(solution)/shard_map/qkv_0/pallas_call | solution.py:494
  93.3 0.0 copy-done.2
  93.3 33.5 %all-gather = s32[32,1,256]{2,1,0:T(1,128)S(1)} all-gather(s32[1,1,256]{2,1,0:T(1,128)S(1)} %bitcast.29), channel_id=1, replica_groups=mesh['dp'=1,'sp'=4,'tp'=8] {'sp','tp'}, dimensions={0}, use_global_device_ids=true | all-gather | bytes 33792 | tf_op jit(solution)/shard_map/all_gather | solution.py:601
  126.8 0.8 fusion.5
  127.6 1.4 maximum_subtract_fusion.1
  129.1 1.4 select_select_fusion.1
  130.5 0.6 stack.5.bounds
  131.1 3.0 maximum_subtract_fusion
  134.1 17.0 %attend.2.m_ref = bf16[2048,256]{1,0:T(8,128)(2,1)} custom-call(s32[5,4]{1,0:T(8,128)} %stack.5.bounds, bf16[2048,256]{1,0:T(8,128)(2,1)} %get-tuple-element.10.q_ref, s32[2048,1]{1,0:T(8,128)} %get-tuple-element.34.lo_ref, bf16[2,4096,256]{2,1,0:T(8,128)(2,1)} %get-tuple-element.11.kv_ref), custom_call_target="tpu_custom_call" | custom-call | tf_op jit(solution)/shard_map/attend/pallas_call | solution.py:565
  151.2 0.0 copy-start.1
  151.2 56.3 %out_0.1.x_ref = bf16[256,2560]{1,0:T(8,128)(2,1)} custom-call(bf16[2048,256]{1,0:T(8,128)(2,1)} %attend.2.m_ref, bf16[256,2560]{1,0:T(8,128)(2,1)} %x_ref.3, bf16[2,256,2560]{2,1,0:T(8,128)(2,1)} %bitcast.27), custom_call_target="tpu_custom_call" | custom-call | tf_op jit(solution)/shard_map/out_0/pallas_call | solution.py:321
  207.5 0.0 copy-done.1
  207.5 0.6 fusion.13
  208.1 113.0 %mlp_0.1.x_ref = bf16[256,2560]{1,0:T(8,128)(2,1)} custom-call(bf16[256,2560]{1,0:T(8,128)(2,1)} %out_0.1.x_ref, bf16[1,2560]{1,0:T(2,128)(2,1)} %get-tuple-element.24.g_ref, bf16[2,2560,1280]{2,1,0:T(8,128)(2,1)} %wg_hbm.3, bf16[2,2560,1280]{2,1,0:T(8,128)(2,1)} %wu_hbm.3, bf16[2,1280,2560]{2,1,0:T(8,128)(2,1)} %wd_hbm.3), custom_call_target="tpu_custom_call" | custom-call | tf_op jit(solution)/shard_map/mlp_0/pallas_call | solution.py:266
  321.1 70.3 %qkv_1.1 = (bf16[2048,256]{1,0:T(8,128)(2,1)}, bf16[2,8192,256]{2,1,0:T(8,128)(2,1)}) custom-call(bf16[256,2560]{1,0:T(8,128)(2,1)} %mlp_0.1.x_ref, bf16[1,2560]{1,0:T(2,128)(2,1)} %get-tuple-element.25.g_ref, f32[4,512,256]{2,1,0:T(8,128)} %get-tuple-element.12.tab_in, bf16[2,2560,256]{2,1,0:T(8,128)(2,1)} %bitcast.26, bf16[2,2560,256]{2,1,0:T(8,128)(2,1)} %fusion.wkv_hbm), custom_call_target="tpu_custom_call" | custom-call | tf_op jit(solution)/shard_map/qkv_1/pallas_call | solution.py:494
  391.5 0.6 stack.4.bounds
  392.1 34.3 %attend.3.m_ref = bf16[2048,256]{1,0:T(8,128)(2,1)} custom-call(s32[5,4]{1,0:T(8,128)} %stack.4.bounds, bf16[2048,256]{1,0:T(8,128)(2,1)} %get-tuple-element.13.q_ref, s32[2048,1]{1,0:T(8,128)} %get-tuple-element.35.lo_ref, bf16[2,8192,256]{2,1,0:T(8,128)(2,1)} %get-tuple-element.14.kv_ref), custom_call_target="tpu_custom_call" | custom-call | tf_op jit(solution)/shard_map/attend/pallas_call | solution.py:565
  426.4 57.6 %out_1.1.x_ref = bf16[256,2560]{1,0:T(8,128)(2,1)} custom-call(bf16[2048,256]{1,0:T(8,128)(2,1)} %attend.3.m_ref, bf16[256,2560]{1,0:T(8,128)(2,1)} %mlp_0.1.x_ref, bf16[2,256,2560]{2,1,0:T(8,128)(2,1)} %bitcast.28), custom_call_target="tpu_custom_call" | custom-call | tf_op jit(solution)/shard_map/out_1/pallas_call | solution.py:321
  484.0 112.2 %mlp_1.1 = bf16[256,2560]{1,0:T(8,128)(2,1)} custom-call(bf16[256,2560]{1,0:T(8,128)(2,1)} %out_1.1.x_ref, bf16[1,2560]{1,0:T(2,128)(2,1)} %get-tuple-element.23.g_ref, bf16[2,2560,1280]{2,1,0:T(8,128)(2,1)} %wg_hbm.3, bf16[2,2560,1280]{2,1,0:T(8,128)(2,1)} %wu_hbm.3, bf16[2,1280,2560]{2,1,0:T(8,128)(2,1)} %wd_hbm.3), custom_call_target="tpu_custom_call" | custom-call | tf_op jit(solution)/shard_map/mlp_1/pallas_call | solution.py:266
  596.2 2.5 copy.24
  (6 shorter events, 0.1 us)
Async XLA Ops:
  13.6 6.2 %copy-start.3 = (s32[256]{0:T(256)S(1)}, s32[256]{0:T(256)}, u32[]{:S(2)}) copy-start(s32[256]{0:T(256)} %param.14) | copy-start | bytes 3076
  13.6 7.5 %copy-start = (bf16[2,2560]{1,0:T(2,128)(2,1)S(1)}, bf16[2,2560]{1,0:T(2,128)(2,1)}, u32[]{:S(2)}) copy-start(bf16[2,2560]{1,0:T(2,128)(2,1)} %param.15) | copy-start | bytes 30724
  19.8 73.5 %copy-start.2 = (s32[256]{0:T(256)S(1)}, s32[256]{0:T(256)}, u32[]{:S(2)}) copy-start(s32[256]{0:T(256)} %param.13) | copy-start | bytes 3076
  151.2 56.3 %copy-start.1 = (bf16[2,2560]{1,0:T(2,128)(2,1)S(1)}, bf16[2,2560]{1,0:T(2,128)(2,1)}, u32[]{:S(2)}) copy-start(bf16[2,2560]{1,0:T(2,128)(2,1)} %param.20) | copy-start | bytes 30724

commit v2 on v1

--- a/solution.py
+++ b/solution.py
@@ -16,8 +16,8 @@
 BF16 = jnp.bfloat16
 F32 = jnp.float32
 VMEM_LIMIT = 66_000_000
-Q_BLOCK = 512
-K_BLOCK = 512
+UP_TILE = 1280
+DOWN_TILE = 2560
 
 
 def _place():
@@ -53,47 +53,57 @@
     elif k == 1:
         chip, h = (x + CHIPS - 1, 0) if even else (x + 1, 1)
     elif k == 2:
+        chip, h = x + 2, j % 2
+    else:
         chip, h = (x + CHIPS - 1, 1) if even else (x + 1, 0)
-    else:
-        chip, h = x + 2, j % 2
     return lax.rem(chip, CHIPS) * (2 * rows) + core * rows + h * half
 
 
 def _gather_copies(buf, sems, rows, right, left, sib):
-    half = rows // 2
+    half, part = rows // 2, rows // 4
     a, b = pl.ds(0, half), pl.ds(half, half)
+    a1, a2, b1, b2 = (pl.ds(i * part, part) for i in range(4))
     ring = [
         _copy(buf.at[0, a], buf.at[1, a], sems, 0, "tp", right),
         _copy(buf.at[0, b], buf.at[1, b], sems, 1, "tp", left),
-        _copy(buf.at[0, b], buf.at[2, a], sems, 2, "tp", right),
-        _copy(buf.at[0, a], buf.at[2, b], sems, 3, "tp", left),
-        _copy(buf.at[1, a], buf.at[3, a], sems, 4, "tp", right),
-        _copy(buf.at[1, b], buf.at[3, b], sems, 5, "tp", left),
+        _copy(buf.at[0, b1], buf.at[3, a1], sems, 2, "tp", right),
+        _copy(buf.at[0, a1], buf.at[3, b1], sems, 3, "tp", left),
+        _copy(buf.at[1, a], buf.at[2, a], sems, 4, "tp", right),
+        _copy(buf.at[1, b], buf.at[2, b], sems, 5, "tp", left),
+        _copy(buf.at[0, b2], buf.at[3, a2], sems, 6, "tp", right),
+        _copy(buf.at[0, a2], buf.at[3, b2], sems, 7, "tp", left),
     ]
-    relay = [_copy(buf.at[k, pl.ds(0, rows)], buf.at[k, pl.ds(rows, rows)], sems, 6 + k, "tp", sib) for k in range(4)]
+    relay = [_copy(buf.at[k, pl.ds(0, rows)], buf.at[k, pl.ds(rows, rows)], sems, 8 + k, "tp", sib) for k in range(4)]
     return ring, relay
 
 
-def _gather_begin(ring, relay):
+def _gather_begin(*gathers):
     for i in (0, 1):
-        ring[i].start()
-    relay[0].start()
+        for ring, relay in gathers:
+            ring[i].start()
+    for ring, relay in gathers:
+        relay[0].start()
     for i in (2, 3):
-        ring[i].start()
-
-
-def _gather_arrive(ring, relay, k):
+        for ring, relay in gathers:
+            ring[i].start()
+
+
+def _gather_arrive(k, *gathers):
     if k == 1:
-        ring[0].wait_recv()
-        ring[4].start()
-        ring[1].wait_recv()
-        ring[5].start()
-    elif k >= 2:
-        ring[2 * k - 2].wait_recv()
-        ring[2 * k - 1].wait_recv()
-    if k >= 1:
-        relay[k].start()
-    relay[k].wait_recv()
+        for i in (0, 1):
+            for ring, relay in gathers:
+                ring[i].wait_recv()
+                ring[4 + i].start()
+        for i in (6, 7):
+            for ring, relay in gathers:
+                ring[i].start()
+    for ring, relay in gathers:
+        for i in {2: (4, 5), 3: (2, 3, 6, 7)}.get(k, ()):
+            ring[i].wait_recv()
+        if k >= 1:
+            relay[k].start()
+    for ring, relay in gathers:
+        relay[k].wait_recv()
 
 
 def _gather_end(ring, relay):
@@ -133,9 +143,9 @@
         self.rows, self.part, self.from_sib = rows, part, from_sib
         self.direct, self.chain, self.last = direct, chain, last
         self.swap = [_copy(part.at[k, pl.ds(rows, rows)], from_sib.at[k], sems, k, "tp", sib) for k in range(4)]
-        self.d = [_copy(part.at[2, b], direct.at[a], sems, 4, "tp", right), _copy(part.at[2, a], direct.at[b], sems, 5, "tp", left)]
-        self.c = [_copy(part.at[3, b], chain.at[b], sems, 6, "tp", right), _copy(part.at[3, a], chain.at[a], sems, 7, "tp", left)]
-        self.l = [_copy(part.at[1, b], last.at[b], sems, 8, "tp", right), _copy(part.at[1, a], last.at[a], sems, 9, "tp", left)]
+        self.d = [_copy(part.at[1, b], direct.at[b], sems, 4, "tp", right), _copy(part.at[1, a], direct.at[a], sems, 5, "tp", left)]
+        self.c = [_copy(part.at[2, a], chain.at[b], sems, 6, "tp", right), _copy(part.at[2, b], chain.at[a], sems, 7, "tp", left)]
+        self.l = [_copy(part.at[3, b], last.at[a], sems, 8, "tp", right), _copy(part.at[3, a], last.at[b], sems, 9, "tp", left)]
 
     def _fold(self, k, extra=None):
         part, from_sib = self.part, self.from_sib
@@ -149,22 +159,22 @@
         _add_rows(self.rows, body)
 
     def send_direct(self):
+        self.swap[1].wait_recv()
+        self._fold(1)
+        for copy in self.d:
+            copy.start()
+
+    def send_chain(self):
         self.swap[2].wait_recv()
         self._fold(2)
-        for copy in self.d:
-            copy.start()
-
-    def send_chain(self):
-        self.swap[3].wait_recv()
-        self._fold(3)
         for copy in self.c:
             copy.start()
 
     def forward_chain(self):
-        self.swap[1].wait_recv()
+        self.swap[3].wait_recv()
         for copy in self.c:
             copy.wait_recv()
-        self._fold(1, self.chain)
+        self._fold(3, self.chain)
         for copy in self.l:
             copy.start()
 
@@ -200,63 +210,70 @@
     return pltpu.CompilerParams(collective_id=collective_id, has_side_effects=True, vmem_limit_bytes=VMEM_LIMIT)
 
 
-def _mlp_kernel(layer, x_ref, g_ref, wg_hbm, wu_hbm, wd_hbm, o_ref, buf, wg, wu, wd, act, part, from_sib, direct, chain, last,
+def _mlp_kernel(layer, x_ref, g_ref, wg_hbm, wu_hbm, wd_hbm, o_ref, buf, wgu, wd, act, part, from_sib, direct, chain, last,
                 s_send, s_recv, g_send, g_recv, w_sem):
     rows, model = x_ref.shape
-    cols = wg.shape[1]
+    cols = act.shape[1]
+    tiles = cols // UP_TILE
     x, c, right, left, sib = _place()
-    loads = [pltpu.make_async_copy(src.at[layer], dst, w_sem.at[i]) for i, (src, dst) in enumerate(((wg_hbm, wg), (wu_hbm, wu), (wd_hbm, wd)))]
-    for load in loads:
-        load.start()
+
+    def load(i, n):
+        src = (wg_hbm, wu_hbm)[i].at[layer, :, pl.ds(n * UP_TILE, UP_TILE)]
+        return pltpu.make_async_copy(src, wgu.at[:, pl.ds((2 * n + i) * UP_TILE, UP_TILE)], w_sem.at[2 * n + i])
+
+    load_down = pltpu.make_async_copy(wd_hbm.at[layer], wd, w_sem.at[2 * tiles])
+    for n in range(tiles):
+        load(0, n).start()
+        load(1, n).start()
+    load_down.start()
     _norm_into(buf, x_ref, g_ref)
     _barrier((("tp", left), ("tp", right), ("tp", sib)))
-    ring, relay = _gather_copies(buf, (g_send, g_recv), rows, right, left, sib)
-    _gather_begin(ring, relay)
+    gather = _gather_copies(buf, (g_send, g_recv), rows, right, left, sib)
+    _gather_begin(gather)
     scatter = _Scatter(part, from_sib, direct, chain, last, (s_send, s_recv), rows, right, left, sib)
-    nt = 256
+    for n in range(tiles):
+        load(0, n).wait()
+        load(1, n).wait()
 
     def step(k, carry):
         for kk in range(4):
             @pl.when(k == kk)
             def _():
-                _gather_arrive(ring, relay, kk)
-                if kk == 0:
-                    loads[0].wait()
-                    loads[1].wait()
+                _gather_arrive(kk, gather)
 
         def up(n, inner):
-            cs = pl.ds(pl.multiple_of(n * nt, nt), nt)
-            gate = jnp.dot(buf[k], wg[:, cs], preferred_element_type=F32)
-            lin = jnp.dot(buf[k], wu[:, cs], preferred_element_type=F32)
-            act[:, cs] = (jax.nn.silu(gate) * lin).astype(BF16)
+            cs = pl.ds(pl.multiple_of(n * 2 * UP_TILE, 2 * UP_TILE), 2 * UP_TILE)
+            both = jnp.dot(buf[k], wgu[:, cs], preferred_element_type=F32)
+            gate, lin = both[:, :UP_TILE], both[:, UP_TILE:]
+            act[:, pl.ds(pl.multiple_of(n * UP_TILE, UP_TILE), UP_TILE)] = (jax.nn.silu(gate) * lin).astype(BF16)
             return inner
 
-        lax.fori_loop(0, cols // nt, up, 0)
+        lax.fori_loop(0, tiles, up, 0)
 
         @pl.when(k == 0)
         def _():
-            loads[2].wait()
+            load_down.wait()
 
         def down(n, inner):
-            cs = pl.ds(pl.multiple_of(n * nt, nt), nt)
+            cs = pl.ds(pl.multiple_of(n * DOWN_TILE, DOWN_TILE), DOWN_TILE)
             part[k, :, cs] = jnp.dot(act[...], wd[:, cs], preferred_element_type=F32).astype(BF16)
             return inner
 
-        lax.fori_loop(0, model // nt, down, 0)
+        lax.fori_loop(0, model // DOWN_TILE, down, 0)
         for kk in range(4):
             @pl.when(k == kk)
             def _():
                 scatter.swap[kk].start()
+                if kk == 1:
+                    scatter.send_direct()
                 if kk == 2:
-                    scatter.send_direct()
-                if kk == 3:
                     scatter.send_chain()
         return carry
 
     lax.fori_loop(0, 4, step, 0)
     scatter.forward_chain()
     scatter.finish(o_ref, x_ref)
-    _gather_end(ring, relay)
+    _gather_end(*gather)
 
 
 def _mlp(layer, x, gain, w_gate, w_up, w_down):
@@ -271,14 +288,13 @@
         out_specs=vmem,
         scratch_shapes=[
             pltpu.VMEM((4, 2 * rows, model), BF16),
-            pltpu.VMEM((model, cols), BF16),
-            pltpu.VMEM((model, cols), BF16),
+            pltpu.VMEM((model, 2 * cols), BF16),
             pltpu.VMEM((cols, model), BF16),
             pltpu.VMEM((2 * rows, cols), BF16),
             *_scatter_scratch(rows, model),
-            pltpu.SemaphoreType.DMA((10,)),
-            pltpu.SemaphoreType.DMA((10,)),
-            pltpu.SemaphoreType.DMA((3,)),
+            pltpu.SemaphoreType.DMA((12,)),
+            pltpu.SemaphoreType.DMA((12,)),
+            pltpu.SemaphoreType.DMA((2 * (cols // UP_TILE) + 1,)),
         ],
         compiler_params=_params(layer),
     )(x, gain, w_gate, w_up, w_down)
@@ -294,7 +310,7 @@
     scatter = _Scatter(part, from_sib, direct, chain, last, (s_send, s_recv), rows, right, left, sib)
     load.wait()
     nt = 512
-    for k in (2, 3, 1, 0):
+    for k in (2, 1, 3, 0):
         for j in range(4):
             start = pl.multiple_of(_piece_rows(x, c, rows, k, j), half)
             lhs[pl.ds(j * half, half), :] = m_ref[pl.ds(start, half), :]
@@ -307,9 +323,9 @@
         lax.fori_loop(0, model // nt, down, 0)
         scatter.swap[k].start()
         if k == 2:
+            scatter.send_chain()
+        if k == 1:
             scatter.send_direct()
-        if k == 3:
-            scatter.send_chain()
     scatter.forward_chain()
     scatter.finish(o_ref, x_ref)
 
@@ -334,9 +350,14 @@
     )(mixed, x, w_o)
 
 
-def _qkv_kernel(layer, gather_tab, windowed, shards, x_ref, g_ref, tab_in, wq_hbm, wkv_hbm, q_out, kv_out, *rest):
+def _qkv_kernel(layer, gather_tab, windowed, shards, x_ref, g_ref, tab_in, wq_hbm, wkv_hbm, *rest):
     if gather_tab:
-        tab_out, rest = rest[0], rest[1:]
+        n_ref, q_out, kv_out, tab_out, n_out = rest[:5]
+        n_y, n_x, n_send, n_recv, c_send, c_recv = rest[5:11]
+        rest = rest[11:]
+    else:
+        q_out, kv_out = rest[:2]
+        rest = rest[2:]
     buf, tab, wq, wkv, qs, kv, g_send, g_recv, t_send, t_recv, y_send, y_recv, p_send, p_recv, l_sem, q_sem, w_sem = rest
     rows, model = x_ref.shape
     half, step_rows = rows // 2, 2 * rows
@@ -355,21 +376,27 @@
         tab_load = pltpu.make_async_copy(tab_in, tab.at[0, pl.ds(0, rows)], w_sem.at[2])
         tab_load.start()
     _norm_into(buf, x_ref, g_ref)
+    if gather_tab:
+        n_y[0] = n_ref[...]
     tab_load.wait()
     _barrier((("tp", left), ("tp", right), ("tp", sib), ("sp", up), ("sp", down)))
-    ring, relay = _gather_copies(buf, (g_send, g_recv), rows, right, left, sib)
+    gather = _gather_copies(buf, (g_send, g_recv), rows, right, left, sib)
+    gathers = [gather]
     if gather_tab:
-        t_ring, t_relay = _gather_copies(tab, (t_send, t_recv), rows, right, left, sib)
-        for i in (0, 1):
-            t_ring[i].start()
-            ring[i].start()
-        t_relay[0].start()
-        relay[0].start()
-        for i in (2, 3):
-            t_ring[i].start()
-            ring[i].start()
-    else:
-        _gather_begin(ring, relay)
+        gathers.insert(0, _gather_copies(tab, (t_send, t_recv), rows, right, left, sib))
+        n_copies = [_copy(n_y.at[src], n_y.at[dst], (c_send, c_recv), i, "sp", dev) for i, (src, dst, dev) in enumerate(((0, 1, up), (0, 2, down), (1, 3, up)))]
+        n_copies[0].start()
+        n_copies[1].start()
+    _gather_begin(*gathers)
+    if gather_tab:
+        n_copies[0].wait_recv()
+        n_copies[2].start()
+        n_copies[1].wait_recv()
+        n_copies[2].wait_recv()
+        n_x[0, :32, :] = jnp.zeros((32, 128), F32)
+        n_x[0, :8, :] = n_y[0] + n_y[1] + n_y[2] + n_y[3]
+        gathers.append(_gather_copies(n_x, (n_send, n_recv), 32, right, left, sib))
+        _gather_begin(gathers[2])
 
     if windowed:
         bases = (shard, 0)
@@ -419,9 +446,7 @@
                 if kk == 0:
                     loads[0].wait()
                     loads[1].wait()
-                if gather_tab:
-                    _gather_arrive(t_ring, t_relay, kk)
-                _gather_arrive(ring, relay, kk)
+                _gather_arrive(kk, *gathers)
 
         cos, sin = tab[k, :, :hd // 2], tab[k, :, hd // 2:]
 
@@ -465,7 +490,14 @@
         store = pltpu.make_async_copy(tab, tab_out, w_sem.at[3])
         store.start()
         store.wait()
-        _gather_end(t_ring, t_relay)
+        total = n_x[0, :8, :]
+        for k in range(4):
+            for i in range(8):
+                if k or i:
+                    total = total + n_x[k, 8 * i:8 * i + 8, :]
+        n_out[...] = total
+        for copy in n_copies:
+            copy.wait_send()
     pltpu.make_async_copy(qs, q_out, q_sem.at[0]).wait()
     for s, base in enumerate(bases):
         span = pl.ds(pl.multiple_of(base, shard), shard)
@@ -477,10 +509,11 @@
         first, second = y_copies(k)
         for copy in first + second:
             copy.wait_send()
-    _gather_end(ring, relay)
-
-
-def _qkv(layer, windowed, shards, x, gain, tab, w_q, w_kv):
+    for ring, relay in gathers:
+        _gather_end(ring, relay)
+
+
+def _qkv(layer, windowed, shards, x, gain, tab, w_q, w_kv, counts):
     rows, model = x.shape
     hd = w_q.shape[2]
     gather_tab = tab.ndim == 2
@@ -490,24 +523,27 @@
     tab_shape = (4, 2 * rows, hd)
     out_shape = [jax.ShapeDtypeStruct((shard, hd), BF16), jax.ShapeDtypeStruct((2, held * shard, hd), BF16)]
     if gather_tab:
-        out_shape.append(jax.ShapeDtypeStruct(tab_shape, F32))
+        out_shape += [jax.ShapeDtypeStruct(tab_shape, F32), jax.ShapeDtypeStruct(counts.shape, F32)]
+    dma = pltpu.SemaphoreType.DMA
+    count_scratch = [pltpu.VMEM((4, *counts.shape), F32), pltpu.VMEM((4, 64, 128), F32), dma((12,)), dma((12,)), dma((3,)), dma((3,))]
     return pl.pallas_call(
         functools.partial(_qkv_kernel, layer, gather_tab, windowed, shards),
         name=f"qkv_{layer}",
         out_shape=out_shape,
-        in_specs=[vmem, vmem, hbm, hbm, hbm],
-        out_specs=[hbm] * len(out_shape),
+        in_specs=[vmem, vmem, hbm, hbm, hbm] + [vmem] * gather_tab,
+        out_specs=[hbm] * 3 + [vmem] if gather_tab else [hbm] * 2,
         scratch_shapes=[
+            *(count_scratch if gather_tab else []),
             pltpu.VMEM((4, 2 * rows, model), BF16),
             pltpu.VMEM(tab_shape, F32),
             pltpu.VMEM((model, hd), BF16),
             pltpu.VMEM((model, hd), BF16),
             pltpu.VMEM((shard, hd), BF16),
             pltpu.VMEM((held, shard, hd), BF16),
-            pltpu.SemaphoreType.DMA((10,)),
-            pltpu.SemaphoreType.DMA((10,)),
-            pltpu.SemaphoreType.DMA((10,)),
-            pltpu.SemaphoreType.DMA((10,)),
+            pltpu.SemaphoreType.DMA((12,)),
+            pltpu.SemaphoreType.DMA((12,)),
+            pltpu.SemaphoreType.DMA((12,)),
+            pltpu.SemaphoreType.DMA((12,)),
             pltpu.SemaphoreType.DMA((16,)),
             pltpu.SemaphoreType.DMA((16,)),
             pltpu.SemaphoreType.DMA((4,)),
@@ -517,10 +553,10 @@
             pltpu.SemaphoreType.DMA((4,)),
         ],
         compiler_params=_params(4 + layer),
-    )(x, gain, tab, w_q, w_kv)
-
-
-def _attend_kernel(scale, bounds, q_ref, lo_ref, kv_ref, o_ref, m_sc, l_sc, acc_sc):
+    )(x, gain, tab, w_q, w_kv, *([counts] if gather_tab else []))
+
+
+def _attend_kernel(scale, k_block, bounds, q_ref, lo_ref, kv_ref, o_ref, m_sc, l_sc, acc_sc):
     i = pl.program_id(0)
     rows, hd = q_ref.shape
     m_sc[...] = jnp.full(m_sc.shape, -1e30, F32)
@@ -529,56 +565,57 @@
     first = bounds[4, i]
 
     def block(masked, b, carry):
-        start = pl.multiple_of(b * K_BLOCK, K_BLOCK)
-        k = kv_ref[0, pl.ds(start, K_BLOCK), :]
-        v = kv_ref[1, pl.ds(start, K_BLOCK), :]
-        s = lax.dot_general(q_ref[...], k, (((1,), (1,)), ((), ())), preferred_element_type=F32)
+        start = pl.multiple_of(b * k_block, k_block)
+        k = kv_ref[0, pl.ds(start, k_block), :]
+        v = kv_ref[1, pl.ds(start, k_block), :]
+        s = lax.dot_general(k, q_ref[...], (((1,), (1,)), ((), ())), preferred_element_type=F32)
         if masked:
-            j = start + lax.broadcasted_iota(jnp.int32, (rows, K_BLOCK), 1)
-            r = first + lax.broadcasted_iota(jnp.int32, (rows, K_BLOCK), 0)
+            j = start + lax.broadcasted_iota(jnp.int32, (k_block, rows), 0)
+            r = first + lax.broadcasted_iota(jnp.int32, (k_block, rows), 1)
             s = jnp.where((j <= r) & (j >= lo_ref[...]), s, -1e30)
         m_old = m_sc[...]
-        m_new = jnp.maximum(m_old, jnp.max(s, axis=1, keepdims=True))
+        m_new = jnp.maximum(m_old, jnp.max(s, axis=0, keepdims=True))
         p = jnp.exp2((s - m_new) * scale)
         alpha = jnp.exp2((m_old - m_new) * scale)
         m_sc[...] = m_new
-        l_sc[...] = l_sc[...] * alpha + jnp.sum(p, axis=1, keepdims=True)
-        acc_sc[...] = acc_sc[...] * alpha + jnp.dot(p.astype(BF16), v, preferred_element_type=F32)
+        l_sc[...] = l_sc[...] * alpha + jnp.sum(p, axis=0, keepdims=True)
+        add = lax.dot_general(v, p.astype(BF16), (((0,), (0,)), ((), ())), preferred_element_type=F32)
+        acc_sc[...] = acc_sc[...] * alpha + add
         return carry
 
     lax.fori_loop(bounds[0, i], bounds[1, i], functools.partial(block, True), 0)
     lax.fori_loop(bounds[1, i], bounds[2, i], functools.partial(block, False), 0)
     lax.fori_loop(bounds[2, i], bounds[3, i], functools.partial(block, True), 0)
-    o_ref[...] = (acc_sc[...] / l_sc[...]).astype(BF16)
-
-
-def _attend(q, kv, row_lo, first_row):
+    o_ref[...] = jnp.transpose(acc_sc[...] / l_sc[...]).astype(BF16)
+
+
+def _attend(q, kv, row_lo, first_row, block):
     total, hd = q.shape
-    blocks = total // Q_BLOCK
-    lo2 = row_lo.reshape(blocks, Q_BLOCK)
-    first = first_row + jnp.arange(blocks, dtype=jnp.int32) * Q_BLOCK
-    b_lo = lo2[:, 0] // K_BLOCK
-    b_hi = (first + Q_BLOCK - 1) // K_BLOCK + 1
-    b_a = jnp.clip((lo2[:, -1] + K_BLOCK - 1) // K_BLOCK, b_lo, b_hi)
-    b_b = jnp.clip((first + 1) // K_BLOCK, b_a, b_hi)
+    blocks = total // block
+    lo2 = row_lo.reshape(blocks, block)
+    first = first_row + jnp.arange(blocks, dtype=jnp.int32) * block
+    b_lo = lo2[:, 0] // block
+    b_hi = (first + block - 1) // block + 1
+    b_a = jnp.clip((lo2[:, -1] + block - 1) // block, b_lo, b_hi)
+    b_b = jnp.clip((first + 1) // block, b_a, b_hi)
     bounds = jnp.stack([b_lo, b_a, b_b, b_hi, first]).astype(jnp.int32)
     return pl.pallas_call(
-        functools.partial(_attend_kernel, hd ** -0.5 * math.log2(math.e)),
+        functools.partial(_attend_kernel, hd ** -0.5 * math.log2(math.e), block),
         name="attend",
         out_shape=jax.ShapeDtypeStruct((total, hd), BF16),
         grid_spec=pltpu.PrefetchScalarGridSpec(
             num_scalar_prefetch=1,
             grid=(blocks,),
             in_specs=[
-                pl.BlockSpec((Q_BLOCK, hd), lambda i, b: (i, 0)),
-                pl.BlockSpec((Q_BLOCK, 1), lambda i, b: (i, 0)),
+                pl.BlockSpec((block, hd), lambda i, b: (i, 0)),
+                pl.BlockSpec((1, block), lambda i, b: (0, i)),
                 pl.BlockSpec(memory_space=pltpu.VMEM),
             ],
-            out_specs=pl.BlockSpec((Q_BLOCK, hd), lambda i, b: (i, 0)),
-            scratch_shapes=[pltpu.VMEM((Q_BLOCK, 1), F32), pltpu.VMEM((Q_BLOCK, 1), F32), pltpu.VMEM((Q_BLOCK, hd), F32)],
+            out_specs=pl.BlockSpec((block, hd), lambda i, b: (i, 0)),
+            scratch_shapes=[pltpu.VMEM((1, block), F32), pltpu.VMEM((1, block), F32), pltpu.VMEM((hd, block), F32)],
         ),
         compiler_params=pltpu.CompilerParams(dimension_semantics=("arbitrary",), vmem_limit_bytes=VMEM_LIMIT),
-    )(bounds, q, row_lo.reshape(total, 1), kv)
+    )(bounds, q, row_lo.reshape(1, total), kv)
 
 
 def solution(mesh):
@@ -598,28 +635,31 @@
         inv_freq = ROPE_BASE ** (-jnp.arange(hd // 2, dtype=F32) / (hd // 2))
         angles = positions.astype(F32)[:, None] * inv_freq[None, :]
         tab = jnp.concatenate([jnp.cos(angles), jnp.sin(angles)], axis=1)
-        seg_all = lax.all_gather(segment_ids, ("sp", "tp"), tiled=True)
-        second, third = jnp.sum(seg_all < 1), jnp.sum(seg_all < 2)
+        lane = lax.broadcasted_iota(jnp.int32, (8, 128), 1)
+        counts = jnp.where(lane == 0, jnp.sum(segment_ids < 1), jnp.where(lane == 1, jnp.sum(segment_ids < 2), 0)).astype(F32)
         token = sp_idx * shard + jnp.arange(shard, dtype=jnp.int32)
-        seg_lo = jnp.where(token >= third, third, jnp.where(token >= second, second, 0)).astype(jnp.int32)
-        pick_k = lax.dynamic_slice_in_dim(w_k, kv_head, 1, 2).reshape(layers, model, hd)
-        pick_v = lax.dynamic_slice_in_dim(w_v, kv_head, 1, 2).reshape(layers, model, hd)
-        w_kv = jnp.where(tp_idx % 2 == 0, pick_k, pick_v)
+
+        def pick(w):
+            return lax.optimization_barrier(lax.dynamic_slice_in_dim(w, kv_head, 1, 2).reshape(layers, model, hd))
+
+        w_kv = lax.cond(tp_idx % 2 == 0, lambda: pick(w_k), lambda: pick(w_v))
         w_q2 = w_q.reshape(layers, model, hd)
         w_o2 = w_o.reshape(layers, hd, model)
         for layer in range(layers):
             windowed = layer % 2 == 0
-            got = _qkv(layer, windowed, shards, x, g_attn[layer:layer + 1], tab, w_q2, w_kv)
+            got = _qkv(layer, windowed, shards, x, g_attn[layer:layer + 1], tab, w_q2, w_kv, counts)
             q, kv = got[0], got[1]
-            if len(got) == 3:
+            if layer == 0:
                 tab = got[2]
+                second, third = got[3][0, 0].astype(jnp.int32), got[3][0, 1].astype(jnp.int32)
+                seg_lo = jnp.where(token >= third, third, jnp.where(token >= second, second, 0))
             if windowed:
                 shift = (sp_idx - 1) * shard
                 row_lo = jnp.maximum(seg_lo, token - (WINDOW - 1)) - shift
             else:
                 shift = 0
                 row_lo = seg_lo
-            mixed = _attend(q, kv, row_lo, sp_idx * shard - shift)
+            mixed = _attend(q, kv, row_lo, sp_idx * shard - shift, 512 if windowed else 1024)
             hidden = _out_proj(layer, mixed, x, w_o2)
             x = _mlp(layer, hidden, g_mlp[layer:layer + 1], w_gate, w_up, w_down)
         return x

time: 609 us -> 516 us (0.85); the launches traced: 599 us -> 520 us
  Pallas kernels: 532 us -> 495 us
  blocking collectives: 33.5 us -> 0 us
  other arithmetic: 14.1 us -> 4.73 us
    all_gather x1 -> x0, blocking collectives: 33.5 us -> none  [local_fn(): seg_all = lax.all_gather(segment_ids, ('sp', 'tp'), tiled=True)]
    pallas_call x2, Pallas kernels: 225 us -> 192 us  [_mlp(): pl.pallas_call(functools.partial(_mlp_kernel, layer), name=f'mlp_{layer}'...]
    dynamic_slice x1 -> x0, local copies, waits for them, and re-layouts: 13.6 us -> none  [local_fn(): lax.dynamic_slice_in_dim(w_v, kv_head, 1, 2).reshape(layers, model, hd)]
    another operation x0 -> x1, local copies, waits for them, and re-layouts: none -> 9.34 us
    pallas_call x2, Pallas kernels: 51.3 us -> 45.2 us  [_attend(): pl.pallas_call(functools.partial(_attend_kernel, hd ** (-0.5) * math.log2...]
where the time goes in v2:
time: 516 us; the launch traced here: 520 us
  Pallas kernels  495 us (96%)
  local copies, waits for them, and re-layouts  19 us (4%)
    pallas_call x2, Pallas kernels, _mlp(): pl.pallas_call(functools.partial(_mlp_kernel, layer), name=f'mlp_{layer}'...  192 us
    pallas_call x2, Pallas kernels, _qkv(): pl.pallas_call(functools.partial(_qkv_kernel, layer, gather_tab, windowed...  146 us
    pallas_call x2, Pallas kernels, _out_proj(): pl.pallas_call(functools.partial(_out_kernel, layer), name=f'out_{layer}'...  112 us
    pallas_call x2, Pallas kernels, _attend(): pl.pallas_call(functools.partial(_attend_kernel, hd ** (-0.5) * math.log2...  45.2 us

profile of v2, /device:TPU:112, one launch (start us, length us, event | category | flops | bytes accessed | tf_op | source)
XLA Modules:
  0.0 519.8 jit_solution(12020635575675332611)
XLA Ops:
  0.0 0.0 copy-start.2
  0.0 0.0 copy-start.3
  0.0 0.0 copy-start
  0.0 12.8 %conditional.1 = (bf16[2,2560,256]{2,1,0:T(8,128)(2,1)}) conditional(s32[]{:T(128)} %convert_element_type.28, (s32[]{:T(128)}, bf16[2,2560,4,256]{3,2,1,0:T(4,128)(2,1)}) %tuple.11, (s32[]{:T(128)}, bf16[2,2560,4,256]{3,2,1,0:T(4,128)(2,1)}) %tuple.12), branch_computations={%region_0.1_spmd, %region_1.2_spmd} | conditional | flops 3 | bytes 26214444 | solution.py:645
  0.0 9.3 %copy.26 = bf16[2,2560,4,256]{3,1,0,2:T(8,128)(2,1)} copy(bf16[2,2560,4,256]{3,2,1,0:T(4,128)(2,1)} %get-tuple-element.47) | data formatting | bytes 20971520 | tf_op jit(solution)/shard_map
  9.4 3.5 dynamic-slice_bitcast_fusion.1
  12.8 0.0 copy-done.2
  12.8 0.5 multiply_cosine_fusion
  13.4 0.7 pad_maximum_fusion.tab_in
  14.1 0.0 copy-done.3
  14.1 0.7 fusion.4
  14.8 0.6 compare_select_fusion.2
  15.5 1.2 select_convert_fusion.rest_0_
  16.7 0.0 copy-done
  16.7 0.6 fusion.11
  17.3 74.0 %qkv_0.1 = (bf16[2048,256]{1,0:T(8,128)(2,1)}, bf16[2,4096,256]{2,1,0:T(8,128)(2,1)}, f32[4,512,256]{2,1,0:T(8,128)}, f32[8,128]{1,0:T(8,128)}) custom-call(bf16[256,2560]{1,0:T(8,128)(2,1)} %x_ref.3, bf16[1,2560]{1,0:T(2,128)(2,1)} %get-tuple-element.59.g_ref, f32[256,256]{1,0:T(8,128)} %pad_maximum_fusion.tab_in, bf16[2,2560,256]{2,1,0:T(8,128)(2,1)} %bitcast.28, ...), custom_call_target="tpu_custom_call" | custom-call | tf_op jit(solution)/shard_map/qkv_0/pallas_call | solution.py:529
  91.3 1.3 fusion.12
  94.0 0.6 compare_select_fusion.1
  94.6 0.1 maximum_subtract_fusion
  94.7 0.6 stack.5.bounds
  95.3 13.8 %attend.2.m_ref = bf16[2048,256]{1,0:T(8,128)(2,1)} custom-call(s32[5,4]{1,0:T(8,128)} %stack.5.bounds, bf16[2048,256]{1,0:T(8,128)(2,1)} %get-tuple-element.27.q_ref, s32[1,2048]{1,0:T(1,128)} %get-tuple-element.65.lo_ref, bf16[2,4096,256]{2,1,0:T(8,128)(2,1)} %get-tuple-element.28.kv_ref), custom_call_target="tpu_custom_call" | custom-call | tf_op jit(solution)/shard_map/attend/pallas_call | solution.py:602
  109.2 56.7 %out_0.1.x_ref = bf16[256,2560]{1,0:T(8,128)(2,1)} custom-call(bf16[2048,256]{1,0:T(8,128)(2,1)} %attend.2.m_ref, bf16[256,2560]{1,0:T(8,128)(2,1)} %x_ref.3, bf16[2,256,2560]{2,1,0:T(8,128)(2,1)} %bitcast.30), custom_call_target="tpu_custom_call" | custom-call | tf_op jit(solution)/shard_map/out_0/pallas_call | solution.py:337
  165.9 0.0 copy-done.1
  165.9 0.6 fusion.10
  166.5 96.7 %mlp_0.1.x_ref = bf16[256,2560]{1,0:T(8,128)(2,1)} custom-call(bf16[256,2560]{1,0:T(8,128)(2,1)} %out_0.1.x_ref, bf16[1,2560]{1,0:T(2,128)(2,1)} %get-tuple-element.57.g_ref, bf16[2,2560,1280]{2,1,0:T(8,128)(2,1)} %wg_hbm.3, bf16[2,2560,1280]{2,1,0:T(8,128)(2,1)} %wu_hbm.3, bf16[2,1280,2560]{2,1,0:T(8,128)(2,1)} %wd_hbm.3), custom_call_target="tpu_custom_call" | custom-call | tf_op jit(solution)/shard_map/mlp_0/pallas_call | solution.py:283
  263.3 71.6 %qkv_1.1 = (bf16[2048,256]{1,0:T(8,128)(2,1)}, bf16[2,8192,256]{2,1,0:T(8,128)(2,1)}) custom-call(bf16[256,2560]{1,0:T(8,128)(2,1)} %mlp_0.1.x_ref, bf16[1,2560]{1,0:T(2,128)(2,1)} %get-tuple-element.58.g_ref, f32[4,512,256]{2,1,0:T(8,128)} %get-tuple-element.29.tab_in, bf16[2,2560,256]{2,1,0:T(8,128)(2,1)} %bitcast.29, ...), custom_call_target="tpu_custom_call" | custom-call | tf_op jit(solution)/shard_map/qkv_1/pallas_call | solution.py:529
  334.9 0.1 select_select_fusion
  335.1 0.6 stack.4.bounds
  335.7 31.4 %attend.3.m_ref = bf16[2048,256]{1,0:T(8,128)(2,1)} custom-call(s32[5,2]{1,0:T(8,128)} %stack.4.bounds, bf16[2048,256]{1,0:T(8,128)(2,1)} %get-tuple-element.30.q_ref, s32[1,2048]{1,0:T(1,128)} %get-tuple-element.64.lo_ref, bf16[2,8192,256]{2,1,0:T(8,128)(2,1)} %get-tuple-element.31.kv_ref), custom_call_target="tpu_custom_call" | custom-call | tf_op jit(solution)/shard_map/attend/pallas_call | solution.py:602
  367.1 55.1 %out_1.1.x_ref = bf16[256,2560]{1,0:T(8,128)(2,1)} custom-call(bf16[2048,256]{1,0:T(8,128)(2,1)} %attend.3.m_ref, bf16[256,2560]{1,0:T(8,128)(2,1)} %mlp_0.1.x_ref, bf16[2,256,2560]{2,1,0:T(8,128)(2,1)} %bitcast.31), custom_call_target="tpu_custom_call" | custom-call | tf_op jit(solution)/shard_map/out_1/pallas_call | solution.py:337
  422.2 95.1 %mlp_1.1 = bf16[256,2560]{1,0:T(8,128)(2,1)} custom-call(bf16[256,2560]{1,0:T(8,128)(2,1)} %out_1.1.x_ref, bf16[1,2560]{1,0:T(2,128)(2,1)} %get-tuple-element.56.g_ref, bf16[2,2560,1280]{2,1,0:T(8,128)(2,1)} %wg_hbm.3, bf16[2,2560,1280]{2,1,0:T(8,128)(2,1)} %wu_hbm.3, bf16[2,1280,2560]{2,1,0:T(8,128)(2,1)} %wd_hbm.3), custom_call_target="tpu_custom_call" | custom-call | tf_op jit(solution)/shard_map/mlp_1/pallas_call | solution.py:283
  517.3 2.5 copy.30
  (8 shorter events, 0.1 us)
Async XLA Ops:
  0.0 12.8 %copy-start.2 = (s32[256]{0:T(256)S(1)}, s32[256]{0:T(256)}, u32[]{:S(2)}) copy-start(s32[256]{0:T(256)} %param.16) | copy-start | bytes 3076
  0.0 14.1 %copy-start.3 = (s32[256]{0:T(256)S(1)}, s32[256]{0:T(256)}, u32[]{:S(2)}) copy-start(s32[256]{0:T(256)} %param.15) | copy-start | bytes 3076
  0.0 16.7 %copy-start = (bf16[2,2560]{1,0:T(2,128)(2,1)S(1)}, bf16[2,2560]{1,0:T(2,128)(2,1)}, u32[]{:S(2)}) copy-start(bf16[2,2560]{1,0:T(2,128)(2,1)} %param.17) | copy-start | bytes 30724
  109.2 56.8 %copy-start.1 = (bf16[2,2560]{1,0:T(2,128)(2,1)S(1)}, bf16[2,2560]{1,0:T(2,128)(2,1)}, u32[]{:S(2)}) copy-start(bf16[2,2560]{1,0:T(2,128)(2,1)} %param.22) | copy-start | bytes 30724

commit v3 on v2

--- a/solution.py
+++ b/solution.py
@@ -17,7 +17,8 @@
 F32 = jnp.float32
 VMEM_LIMIT = 66_000_000
 UP_TILE = 1280
-DOWN_TILE = 2560
+DOWN_TILE = 1280
+OUT_TILE = 1280
 
 
 def _place():
@@ -37,11 +38,14 @@
         device_id={axis: dev}, device_id_type=MESH)
 
 
-def _barrier(peers):
+def _greet(peers):
     bar = pltpu.get_barrier_semaphore()
     for axis, dev in peers:
         pl.semaphore_signal(bar, inc=1, device_id={axis: dev}, device_id_type=MESH)
-    pl.semaphore_wait(bar, len(peers))
+
+
+def _meet(peers):
+    pl.semaphore_wait(pltpu.get_barrier_semaphore(), len(peers))
 
 
 def _piece_rows(x, c, rows, k, j):
@@ -102,6 +106,9 @@
             ring[i].wait_recv()
         if k >= 1:
             relay[k].start()
+
+
+def _relay_arrive(k, *gathers):
     for ring, relay in gathers:
         relay[k].wait_recv()
 
@@ -210,49 +217,73 @@
     return pltpu.CompilerParams(collective_id=collective_id, has_side_effects=True, vmem_limit_bytes=VMEM_LIMIT)
 
 
-def _mlp_kernel(layer, x_ref, g_ref, wg_hbm, wu_hbm, wd_hbm, o_ref, buf, wgu, wd, act, part, from_sib, direct, chain, last,
-                s_send, s_recv, g_send, g_recv, w_sem):
+def _block_kernel(layer, m_hbm, x_ref, g_ref, wo_hbm, wg_hbm, wu_hbm, wd_hbm, o_ref, wo, lhs, buf, wgu, wd, act,
+                  part, from_sib, direct, chain, last, s_send, s_recv, o_send, o_recv, g_send, g_recv, w_sem):
     rows, model = x_ref.shape
+    half = rows // 2
     cols = act.shape[1]
-    tiles = cols // UP_TILE
     x, c, right, left, sib = _place()
-
-    def load(i, n):
-        src = (wg_hbm, wu_hbm)[i].at[layer, :, pl.ds(n * UP_TILE, UP_TILE)]
-        return pltpu.make_async_copy(src, wgu.at[:, pl.ds((2 * n + i) * UP_TILE, UP_TILE)], w_sem.at[2 * n + i])
-
-    load_down = pltpu.make_async_copy(wd_hbm.at[layer], wd, w_sem.at[2 * tiles])
-    for n in range(tiles):
-        load(0, n).start()
-        load(1, n).start()
-    load_down.start()
-    _norm_into(buf, x_ref, g_ref)
-    _barrier((("tp", left), ("tp", right), ("tp", sib)))
+    peers = (("tp", left), ("tp", right), ("tp", sib))
+    _greet(peers)
+    loads = [
+        pltpu.make_async_copy(wo_hbm.at[layer], wo, w_sem.at[0]),
+        pltpu.make_async_copy(wg_hbm.at[layer], wgu.at[:, pl.ds(0, cols)], w_sem.at[1]),
+        pltpu.make_async_copy(wu_hbm.at[layer], wgu.at[:, pl.ds(cols, cols)], w_sem.at[2]),
+        pltpu.make_async_copy(wd_hbm.at[layer], wd, w_sem.at[3]),
+    ]
+    loads[0].start()
+    order = (2, 1, 3, 0)
+    for k in order:
+        for j in range(4):
+            start = pl.multiple_of(_piece_rows(x, c, rows, k, j), half)
+            pltpu.make_async_copy(m_hbm.at[pl.ds(start, half)], lhs.at[k, pl.ds(j * half, half)], w_sem.at[4 + k]).start()
+    for load in loads[1:]:
+        load.start()
+    buffers = (part, from_sib, direct, chain, last)
+    scatter = _Scatter(*buffers, (o_send, o_recv), rows, right, left, sib)
+    loads[0].wait()
+    for k in order:
+        pltpu.make_async_copy(m_hbm.at[pl.ds(0, 2 * rows)], lhs.at[k], w_sem.at[4 + k]).wait()
+
+        def project(n, inner):
+            cs = pl.ds(pl.multiple_of(n * OUT_TILE, OUT_TILE), OUT_TILE)
+            part[k, :, cs] = jnp.dot(lhs[k], wo[:, cs], preferred_element_type=F32).astype(BF16)
+            return inner
+
+        lax.fori_loop(0, model // OUT_TILE, project, 0)
+        if k == order[0]:
+            _meet(peers)
+        scatter.swap[k].start()
+        if k == 2:
+            scatter.send_chain()
+        if k == 1:
+            scatter.send_direct()
+    scatter.forward_chain()
+    scatter.finish(o_ref, x_ref)
+
+    _norm_into(buf, o_ref, g_ref)
     gather = _gather_copies(buf, (g_send, g_recv), rows, right, left, sib)
     _gather_begin(gather)
-    scatter = _Scatter(part, from_sib, direct, chain, last, (s_send, s_recv), rows, right, left, sib)
-    for n in range(tiles):
-        load(0, n).wait()
-        load(1, n).wait()
+    scatter = _Scatter(*buffers, (s_send, s_recv), rows, right, left, sib)
+    for load in loads[1:]:
+        load.wait()
 
     def step(k, carry):
         for kk in range(4):
             @pl.when(k == kk)
             def _():
                 _gather_arrive(kk, gather)
+                _relay_arrive(kk, gather)
 
         def up(n, inner):
-            cs = pl.ds(pl.multiple_of(n * 2 * UP_TILE, 2 * UP_TILE), 2 * UP_TILE)
-            both = jnp.dot(buf[k], wgu[:, cs], preferred_element_type=F32)
-            gate, lin = both[:, :UP_TILE], both[:, UP_TILE:]
-            act[:, pl.ds(pl.multiple_of(n * UP_TILE, UP_TILE), UP_TILE)] = (jax.nn.silu(gate) * lin).astype(BF16)
+            cs = pl.ds(pl.multiple_of(n * UP_TILE, UP_TILE), UP_TILE)
+            us = pl.ds(pl.multiple_of(cols + n * UP_TILE, UP_TILE), UP_TILE)
+            gate = jnp.dot(buf[k], wgu[:, cs], preferred_element_type=F32)
+            lin = jnp.dot(buf[k], wgu[:, us], preferred_element_type=F32)
+            act[:, cs] = (jax.nn.silu(gate) * lin).astype(BF16)
             return inner
 
-        lax.fori_loop(0, tiles, up, 0)
-
-        @pl.when(k == 0)
-        def _():
-            load_down.wait()
+        lax.fori_loop(0, cols // UP_TILE, up, 0)
 
         def down(n, inner):
             cs = pl.ds(pl.multiple_of(n * DOWN_TILE, DOWN_TILE), DOWN_TILE)
@@ -272,82 +303,33 @@
 
     lax.fori_loop(0, 4, step, 0)
     scatter.forward_chain()
-    scatter.finish(o_ref, x_ref)
+    scatter.finish(o_ref, o_ref)
     _gather_end(*gather)
 
 
-def _mlp(layer, x, gain, w_gate, w_up, w_down):
+def _block(layer, mixed, x, gain, w_o, w_gate, w_up, w_down):
     rows, model = x.shape
-    cols = w_gate.shape[2]
+    hd, cols = mixed.shape[1], w_gate.shape[2]
     vmem, hbm = pl.BlockSpec(memory_space=pltpu.VMEM), pl.BlockSpec(memory_space=pl.ANY)
+    dma = pltpu.SemaphoreType.DMA
     return pl.pallas_call(
-        functools.partial(_mlp_kernel, layer),
-        name=f"mlp_{layer}",
+        functools.partial(_block_kernel, layer),
+        name=f"block_{layer}",
         out_shape=jax.ShapeDtypeStruct((rows, model), BF16),
-        in_specs=[vmem, vmem, hbm, hbm, hbm],
+        in_specs=[hbm, vmem, vmem, hbm, hbm, hbm, hbm],
         out_specs=vmem,
         scratch_shapes=[
+            pltpu.VMEM((hd, model), BF16),
+            pltpu.VMEM((4, 2 * rows, hd), BF16),
             pltpu.VMEM((4, 2 * rows, model), BF16),
             pltpu.VMEM((model, 2 * cols), BF16),
             pltpu.VMEM((cols, model), BF16),
             pltpu.VMEM((2 * rows, cols), BF16),
             *_scatter_scratch(rows, model),
-            pltpu.SemaphoreType.DMA((12,)),
-            pltpu.SemaphoreType.DMA((12,)),
-            pltpu.SemaphoreType.DMA((2 * (cols // UP_TILE) + 1,)),
+            dma((10,)), dma((10,)), dma((12,)), dma((12,)), dma((8,)),
         ],
         compiler_params=_params(layer),
-    )(x, gain, w_gate, w_up, w_down)
-
-
-def _out_kernel(layer, m_ref, x_ref, wo_hbm, o_ref, wo, lhs, part, from_sib, direct, chain, last, s_send, s_recv, w_sem):
-    rows, model = x_ref.shape
-    half = rows // 2
-    x, c, right, left, sib = _place()
-    load = pltpu.make_async_copy(wo_hbm.at[layer], wo, w_sem.at[0])
-    load.start()
-    _barrier((("tp", left), ("tp", right), ("tp", sib)))
-    scatter = _Scatter(part, from_sib, direct, chain, last, (s_send, s_recv), rows, right, left, sib)
-    load.wait()
-    nt = 512
-    for k in (2, 1, 3, 0):
-        for j in range(4):
-            start = pl.multiple_of(_piece_rows(x, c, rows, k, j), half)
-            lhs[pl.ds(j * half, half), :] = m_ref[pl.ds(start, half), :]
-
-        def down(n, inner):
-            cs = pl.ds(pl.multiple_of(n * nt, nt), nt)
-            part[k, :, cs] = jnp.dot(lhs[...], wo[:, cs], preferred_element_type=F32).astype(BF16)
-            return inner
-
-        lax.fori_loop(0, model // nt, down, 0)
-        scatter.swap[k].start()
-        if k == 2:
-            scatter.send_chain()
-        if k == 1:
-            scatter.send_direct()
-    scatter.forward_chain()
-    scatter.finish(o_ref, x_ref)
-
-
-def _out_proj(layer, mixed, x, w_o):
-    rows, model = x.shape
-    head_dim = mixed.shape[1]
-    vmem, hbm = pl.BlockSpec(memory_space=pltpu.VMEM), pl.BlockSpec(memory_space=pl.ANY)
-    return pl.pallas_call(
-        functools.partial(_out_kernel, layer),
-        name=f"out_{layer}",
-        out_shape=jax.ShapeDtypeStruct((rows, model), BF16),
-        in_specs=[vmem, vmem, hbm],
-        out_specs=vmem,
-        scratch_shapes=[
-            pltpu.VMEM((head_dim, model), BF16),
-            pltpu.VMEM((2 * rows, head_dim), BF16),
-            *_scatter_scratch(rows, model),
-            pltpu.SemaphoreType.DMA((1,)),
-        ],
-        compiler_params=_params(2 + layer),
-    )(mixed, x, w_o)
+    )(mixed, x, gain, w_o, w_gate, w_up, w_down)
 
 
 def _qkv_kernel(layer, gather_tab, windowed, shards, x_ref, g_ref, tab_in, wq_hbm, wkv_hbm, *rest):
@@ -366,6 +348,8 @@
     x, c, right, left, sib = _place()
     y = lax.axis_index("sp")
     up, down = lax.rem(y + 1, shards), lax.rem(y + shards - 1, shards)
+    peers = (("tp", left), ("tp", right), ("tp", sib), ("sp", up), ("sp", down))
+    _greet(peers)
     loads = [pltpu.make_async_copy(wq_hbm.at[layer], wq, w_sem.at[0]), pltpu.make_async_copy(wkv_hbm.at[layer], wkv, w_sem.at[1])]
     for load in loads:
         load.start()
@@ -379,7 +363,7 @@
     if gather_tab:
         n_y[0] = n_ref[...]
     tab_load.wait()
-    _barrier((("tp", left), ("tp", right), ("tp", sib), ("sp", up), ("sp", down)))
+    _meet(peers)
     gather = _gather_copies(buf, (g_send, g_recv), rows, right, left, sib)
     gathers = [gather]
     if gather_tab:
@@ -404,18 +388,20 @@
         bases = tuple(lax.rem(y + d, shards) * shard for d in (0, shards - 1, 1, 2))
 
     def y_copies(k):
-        whole, a, b = pl.ds(k * step_rows, step_rows), pl.ds(k * step_rows, rows), pl.ds(k * step_rows + rows, rows)
+        a, b = pl.ds(k * step_rows, rows), pl.ds(k * step_rows + rows, rows)
         sems = (y_send, y_recv)
-        first = [_copy(kv.at[0, whole], kv.at[1, whole], sems, 4 * k, "sp", up)]
-        second = []
+        first, second = [], []
+        for i, part in enumerate((a, b)):
+            first.append([_copy(kv.at[0, part], kv.at[1, part], sems, 6 * k + 2 * i, "sp", up)])
+            if not windowed:
+                first[i].append(_copy(kv.at[0, part], kv.at[2, part], sems, 6 * k + 2 * i + 1, "sp", down))
         if not windowed:
-            first.append(_copy(kv.at[0, whole], kv.at[2, whole], sems, 4 * k + 1, "sp", down))
-            second.append(_copy(kv.at[1, a], kv.at[3, a], sems, 4 * k + 2, "sp", up))
-            second.append(_copy(kv.at[2, b], kv.at[3, b], sems, 4 * k + 3, "sp", down))
+            second.append(_copy(kv.at[1, a], kv.at[3, a], sems, 6 * k + 4, "sp", up))
+            second.append(_copy(kv.at[2, b], kv.at[3, b], sems, 6 * k + 5, "sp", down))
         return first, second
 
-    def place(s, k):
-        for j in range(4):
+    def place(s, k, js=range(4)):
+        for j in js:
             src = kv.at[s, pl.ds(k * step_rows + j * half, half)]
             start = pl.multiple_of(bases[s] + _piece_rows(x, c, rows, k, j), half)
             dst = kv_out.at[c, pl.ds(start, half)]
@@ -424,13 +410,16 @@
 
     def forward(k):
         first, second = y_copies(k)
-        for copy in first:
-            copy.wait_recv()
-        for copy in second:
-            copy.start()
+        first[0][0].wait_recv()
+        if not windowed:
+            second[0].start()
+        first[1][0].wait_recv()
+        if not windowed:
+            first[1][1].wait_recv()
+            second[1].start()
+            first[0][1].wait_recv()
+            place(2, k)
         place(1, k)
-        if not windowed:
-            place(2, k)
 
     def opposite(k):
         first, second = y_copies(k)
@@ -448,34 +437,49 @@
                     loads[1].wait()
                 _gather_arrive(kk, *gathers)
 
-        cos, sin = tab[k, :, :hd // 2], tab[k, :, hd // 2:]
-
-        def rotate(t):
-            lower, upper = t[:, :hd // 2], t[:, hd // 2:]
-            return jnp.concatenate([lower * cos - upper * sin, upper * cos + lower * sin], axis=-1).astype(BF16)
-
-        q = jnp.dot(buf[k], wq[...], preferred_element_type=F32).astype(BF16).astype(F32)
-        rs = pl.ds(pl.multiple_of(k * step_rows, step_rows), step_rows)
-        qs[rs, :] = rotate(q)
-        t = jnp.dot(buf[k], wkv[...], preferred_element_type=F32).astype(BF16)
-
-        @pl.when(c == 0)
-        def _():
-            kv[0, rs, :] = rotate(t.astype(F32))
-
-        @pl.when(c == 1)
-        def _():
-            kv[0, rs, :] = t
-
+        def part(h, inner):
+            for kk in range(4):
+                @pl.when((k == kk) & (h == 1))
+                def _():
+                    _relay_arrive(kk, *gathers)
+
+            ps = pl.ds(pl.multiple_of(h * rows, rows), rows)
+            rs = pl.ds(pl.multiple_of(k * step_rows + h * rows, rows), rows)
+            cos, sin = tab[k, ps, :hd // 2], tab[k, ps, hd // 2:]
+
+            def rotate(t):
+                lower, upper = t[:, :hd // 2], t[:, hd // 2:]
+                return jnp.concatenate([lower * cos - upper * sin, upper * cos + lower * sin], axis=-1).astype(BF16)
+
+            t = jnp.dot(buf[k, ps, :], wkv[...], preferred_element_type=F32).astype(BF16)
+
+            @pl.when(c == 0)
+            def _():
+                kv[0, rs, :] = rotate(t.astype(F32))
+
+            @pl.when(c == 1)
+            def _():
+                kv[0, rs, :] = t
+
+            for kk in range(4):
+                for hh in range(2):
+                    @pl.when((k == kk) & (h == hh))
+                    def _():
+                        for copy in y_copies(kk)[0][hh]:
+                            copy.start()
+                        place(0, kk, (2 * hh, 2 * hh + 1))
+
+            q = jnp.dot(buf[k, ps, :], wq[...], preferred_element_type=F32).astype(BF16).astype(F32)
+            qs[rs, :] = rotate(q)
+            return inner
+
+        lax.fori_loop(0, 2, part, 0)
         for kk in range(4):
             @pl.when(k == kk)
             def _():
-                for copy in y_copies(kk)[0]:
-                    copy.start()
                 for j in range(4):
                     start = pl.multiple_of(_piece_rows(x, c, rows, kk, j), half)
                     pltpu.make_async_copy(qs.at[pl.ds(kk * step_rows + j * half, half)], q_out.at[pl.ds(start, half)], q_sem.at[0]).start()
-                place(0, kk)
                 if kk >= 1:
                     forward(kk - 1)
                 if kk >= 2:
@@ -507,7 +511,7 @@
         swap.wait_recv()
     for k in range(4):
         first, second = y_copies(k)
-        for copy in first + second:
+        for copy in first[0] + first[1] + second:
             copy.wait_send()
     for ring, relay in gathers:
         _gather_end(ring, relay)
@@ -544,8 +548,8 @@
             pltpu.SemaphoreType.DMA((12,)),
             pltpu.SemaphoreType.DMA((12,)),
             pltpu.SemaphoreType.DMA((12,)),
-            pltpu.SemaphoreType.DMA((16,)),
-            pltpu.SemaphoreType.DMA((16,)),
+            pltpu.SemaphoreType.DMA((24,)),
+            pltpu.SemaphoreType.DMA((24,)),
             pltpu.SemaphoreType.DMA((4,)),
             pltpu.SemaphoreType.DMA((4,)),
             pltpu.SemaphoreType.DMA((4,)),
@@ -639,6 +643,7 @@
         counts = jnp.where(lane == 0, jnp.sum(segment_ids < 1), jnp.where(lane == 1, jnp.sum(segment_ids < 2), 0)).astype(F32)
         token = sp_idx * shard + jnp.arange(shard, dtype=jnp.int32)
 
+
         def pick(w):
             return lax.optimization_barrier(lax.dynamic_slice_in_dim(w, kv_head, 1, 2).reshape(layers, model, hd))
 
@@ -660,8 +665,7 @@
                 shift = 0
                 row_lo = seg_lo
             mixed = _attend(q, kv, row_lo, sp_idx * shard - shift, 512 if windowed else 1024)
-            hidden = _out_proj(layer, mixed, x, w_o2)
-            x = _mlp(layer, hidden, g_mlp[layer:layer + 1], w_gate, w_up, w_down)
+            x = _block(layer, mixed, x, g_mlp[layer:layer + 1], w_o2, w_gate, w_up, w_down)
         return x
 
     return jax.shard_map(local_fn, mesh=mesh, in_specs=in_specs, out_specs=row_spec, check_vma=False)

time: 516 us -> 498 us (0.965)
  Pallas kernels: 495 us -> 477 us
    pallas_call x2, Pallas kernels: 146 us -> 136 us  [_qkv(): pl.pallas_call(functools.partial(_qkv_kernel, layer, gather_tab, windowed...]
    pallas_call x4 -> x2, Pallas kernels: 304 us -> 294 us  [_block(): pl.pallas_call(functools.partial(_block_kernel, layer), name=f'block_{lay...]
where the time goes in v3:
time: 498 us; the launch traced here: 502 us
  Pallas kernels  477 us (96%)
  local copies, waits for them, and re-layouts  19 us (4%)
    pallas_call x2, Pallas kernels, _block(): pl.pallas_call(functools.partial(_block_kernel, layer), name=f'block_{lay...  294 us
    pallas_call x2, Pallas kernels, _qkv(): pl.pallas_call(functools.partial(_qkv_kernel, layer, gather_tab, windowed...  136 us
    pallas_call x2, Pallas kernels, _attend(): pl.pallas_call(functools.partial(_attend_kernel, hd ** (-0.5) * math.log2...  46.1 us

profile of v3, /device:TPU:112, one launch (start us, length us, event | category | flops | bytes accessed | tf_op | source)
XLA Modules:
  0.0 501.9 jit_solution(5486329813179476964)
XLA Ops:
  0.0 0.0 copy-start.2
  0.0 0.0 copy-start.3
  0.0 0.0 copy-start
  0.0 12.8 %conditional.1 = (bf16[2,2560,256]{2,1,0:T(8,128)(2,1)}) conditional(s32[]{:T(128)} %convert_element_type.28, (s32[]{:T(128)}, bf16[2,2560,4,256]{3,2,1,0:T(4,128)(2,1)}) %tuple.11, (s32[]{:T(128)}, bf16[2,2560,4,256]{3,2,1,0:T(4,128)(2,1)}) %tuple.12), branch_computations={%region_0.1_spmd, %region_1.2_spmd} | conditional | flops 3 | bytes 26214444 | solution.py:650
  0.0 9.3 %copy.26 = bf16[2,2560,4,256]{3,1,0,2:T(8,128)(2,1)} copy(bf16[2,2560,4,256]{3,2,1,0:T(4,128)(2,1)} %get-tuple-element.47) | data formatting | bytes 20971520 | tf_op jit(solution)/shard_map
  9.4 3.5 dynamic-slice_bitcast_fusion.1
  12.8 0.0 copy-done.2
  12.8 0.5 multiply_cosine_fusion
  13.4 0.7 pad_maximum_fusion.tab_in
  14.1 0.0 copy-done.3
  14.1 0.7 fusion.4
  14.8 0.6 compare_select_fusion.2
  15.5 1.2 select_convert_fusion.rest_0_
  16.7 0.0 copy-done
  16.7 0.6 fusion.11
  17.3 68.3 %qkv_0.1 = (bf16[2048,256]{1,0:T(8,128)(2,1)}, bf16[2,4096,256]{2,1,0:T(8,128)(2,1)}, f32[4,512,256]{2,1,0:T(8,128)}, f32[8,128]{1,0:T(8,128)}) custom-call(bf16[256,2560]{1,0:T(8,128)(2,1)} %x_ref.3, bf16[1,2560]{1,0:T(2,128)(2,1)} %get-tuple-element.59.g_ref, f32[256,256]{1,0:T(8,128)} %pad_maximum_fusion.tab_in, bf16[2,2560,256]{2,1,0:T(8,128)(2,1)} %bitcast.30, ...), custom_call_target="tpu_custom_call" | custom-call | tf_op jit(solution)/shard_map/qkv_0/pallas_call | solution.py:533
  85.6 1.3 fusion.12
  88.2 0.6 compare_select_fusion.1
  88.9 0.1 maximum_subtract_fusion
  89.0 0.6 stack.5.bounds
  89.6 0.0 copy-start.1
  89.6 14.7 %attend.2.m_hbm = bf16[2048,256]{1,0:T(8,128)(2,1)} custom-call(s32[5,4]{1,0:T(8,128)} %stack.5.bounds, bf16[2048,256]{1,0:T(8,128)(2,1)} %get-tuple-element.27.q_ref, s32[1,2048]{1,0:T(1,128)} %get-tuple-element.65.lo_ref, bf16[2,4096,256]{2,1,0:T(8,128)(2,1)} %get-tuple-element.28.kv_ref), custom_call_target="tpu_custom_call" | custom-call | tf_op jit(solution)/shard_map/attend/pallas_call | solution.py:606
  104.3 0.0 copy-done.1
  104.4 0.6 fusion.10
  105.0 147.7 %block_0.1.x_ref = bf16[256,2560]{1,0:T(8,128)(2,1)} custom-call(bf16[2048,256]{1,0:T(8,128)(2,1)} %attend.2.m_hbm, bf16[256,2560]{1,0:T(8,128)(2,1)} %x_ref.3, bf16[1,2560]{1,0:T(2,128)(2,1)} %get-tuple-element.57.g_ref, bf16[2,256,2560]{2,1,0:T(8,128)(2,1)} %bitcast.28, bf16[2,2560,1280]{2,1,0:T(8,128)(2,1)} %wg_hbm.3, bf16[2,2560,1280]{2,1,0:T(8,128)(2,1)} %wu_hbm.3, ...), custom_call_target="tpu_custom_call" | custom-call | tf_op jit(solution)/shard_map/block_0/pallas_call | solution.py:315
  252.7 67.9 %qkv_1.1 = (bf16[2048,256]{1,0:T(8,128)(2,1)}, bf16[2,8192,256]{2,1,0:T(8,128)(2,1)}) custom-call(bf16[256,2560]{1,0:T(8,128)(2,1)} %block_0.1.x_ref, bf16[1,2560]{1,0:T(2,128)(2,1)} %get-tuple-element.58.g_ref, f32[4,512,256]{2,1,0:T(8,128)} %get-tuple-element.29.tab_in, bf16[2,2560,256]{2,1,0:T(8,128)(2,1)} %bitcast.31, ...), custom_call_target="tpu_custom_call" | custom-call | tf_op jit(solution)/shard_map/qkv_1/pallas_call | solution.py:533
  320.5 0.1 select_select_fusion
  320.7 0.6 stack.4.bounds
  321.3 31.4 %attend.3.m_hbm = bf16[2048,256]{1,0:T(8,128)(2,1)} custom-call(s32[5,2]{1,0:T(8,128)} %stack.4.bounds, bf16[2048,256]{1,0:T(8,128)(2,1)} %get-tuple-element.30.q_ref, s32[1,2048]{1,0:T(1,128)} %get-tuple-element.64.lo_ref, bf16[2,8192,256]{2,1,0:T(8,128)(2,1)} %get-tuple-element.31.kv_ref), custom_call_target="tpu_custom_call" | custom-call | tf_op jit(solution)/shard_map/attend/pallas_call | solution.py:606
  352.7 146.7 %block_1.1 = bf16[256,2560]{1,0:T(8,128)(2,1)} custom-call(bf16[2048,256]{1,0:T(8,128)(2,1)} %attend.3.m_hbm, bf16[256,2560]{1,0:T(8,128)(2,1)} %block_0.1.x_ref, bf16[1,2560]{1,0:T(2,128)(2,1)} %get-tuple-element.56.g_ref, bf16[2,256,2560]{2,1,0:T(8,128)(2,1)} %bitcast.29, bf16[2,2560,1280]{2,1,0:T(8,128)(2,1)} %wg_hbm.3, bf16[2,2560,1280]{2,1,0:T(8,128)(2,1)} %wu_hbm.3, ...), custom_call_target="tpu_custom_call" | custom-call | tf_op jit(solution)/shard_map/block_1/pallas_call | solution.py:315
  499.5 2.5 copy.30
  (7 shorter events, 0.1 us)
Async XLA Ops:
  0.0 12.8 %copy-start.2 = (s32[256]{0:T(256)S(1)}, s32[256]{0:T(256)}, u32[]{:S(2)}) copy-start(s32[256]{0:T(256)} %param.16) | copy-start | bytes 3076
  0.0 14.1 %copy-start.3 = (s32[256]{0:T(256)S(1)}, s32[256]{0:T(256)}, u32[]{:S(2)}) copy-start(s32[256]{0:T(256)} %param.15) | copy-start | bytes 3076
  0.0 16.7 %copy-start = (bf16[2,2560]{1,0:T(2,128)(2,1)S(1)}, bf16[2,2560]{1,0:T(2,128)(2,1)}, u32[]{:S(2)}) copy-start(bf16[2,2560]{1,0:T(2,128)(2,1)} %param.17) | copy-start | bytes 30724
  89.6 14.7 %copy-start.1 = (bf16[2,2560]{1,0:T(2,128)(2,1)S(1)}, bf16[2,2560]{1,0:T(2,128)(2,1)}, u32[]{:S(2)}) copy-start(bf16[2,2560]{1,0:T(2,128)(2,1)} %param.22) | copy-start | bytes 30724

commit v4 on v3

--- a/solution.py
+++ b/solution.py
@@ -118,9 +118,9 @@
         copy.wait_send()
 
 
-def _norm_into(dst, x_ref, g_ref):
+def _norm_into(dst, x_ref, g_ref, layer):
     rows = x_ref.shape[0]
-    gain = g_ref[...].astype(F32)
+    gain = g_ref[layer:layer + 1, :].astype(F32)
     chunk = 16
 
     def body(i, carry):
@@ -261,7 +261,7 @@
     scatter.forward_chain()
     scatter.finish(o_ref, x_ref)
 
-    _norm_into(buf, o_ref, g_ref)
+    _norm_into(buf, o_ref, g_ref, layer)
     gather = _gather_copies(buf, (g_send, g_recv), rows, right, left, sib)
     _gather_begin(gather)
     scatter = _Scatter(*buffers, (s_send, s_recv), rows, right, left, sib)
@@ -359,9 +359,12 @@
     else:
         tab_load = pltpu.make_async_copy(tab_in, tab.at[0, pl.ds(0, rows)], w_sem.at[2])
         tab_load.start()
-    _norm_into(buf, x_ref, g_ref)
+    _norm_into(buf, x_ref, g_ref, layer)
     if gather_tab:
-        n_y[0] = n_ref[...]
+        ids = n_ref[...]
+        n_y[0] = jnp.zeros(n_y.shape[1:], F32)
+        n_y[0, 0:2, :] = jnp.where(ids < 1, 1.0, 0.0)
+        n_y[0, 2:4, :] = jnp.where(ids < 2, 1.0, 0.0)
     tab_load.wait()
     _meet(peers)
     gather = _gather_copies(buf, (g_send, g_recv), rows, right, left, sib)
@@ -527,9 +530,9 @@
     tab_shape = (4, 2 * rows, hd)
     out_shape = [jax.ShapeDtypeStruct((shard, hd), BF16), jax.ShapeDtypeStruct((2, held * shard, hd), BF16)]
     if gather_tab:
-        out_shape += [jax.ShapeDtypeStruct(tab_shape, F32), jax.ShapeDtypeStruct(counts.shape, F32)]
+        out_shape += [jax.ShapeDtypeStruct(tab_shape, F32), jax.ShapeDtypeStruct((8, 128), F32)]
     dma = pltpu.SemaphoreType.DMA
-    count_scratch = [pltpu.VMEM((4, *counts.shape), F32), pltpu.VMEM((4, 64, 128), F32), dma((12,)), dma((12,)), dma((3,)), dma((3,))]
+    count_scratch = [pltpu.VMEM((4, 8, 128), F32), pltpu.VMEM((4, 64, 128), F32), dma((12,)), dma((12,)), dma((3,)), dma((3,))]
     return pl.pallas_call(
         functools.partial(_qkv_kernel, layer, gather_tab, windowed, shards),
         name=f"qkv_{layer}",
@@ -560,13 +563,26 @@
     )(x, gain, tab, w_q, w_kv, *([counts] if gather_tab else []))
 
 
-def _attend_kernel(scale, k_block, bounds, q_ref, lo_ref, kv_ref, o_ref, m_sc, l_sc, acc_sc):
+def _attend_kernel(scale, k_block, window, marks, q_ref, kv_ref, o_ref, m_sc, l_sc, acc_sc):
     i = pl.program_id(0)
     rows, hd = q_ref.shape
     m_sc[...] = jnp.full(m_sc.shape, -1e30, F32)
     l_sc[...] = jnp.zeros(l_sc.shape, F32)
     acc_sc[...] = jnp.zeros(acc_sc.shape, F32)
-    first = bounds[4, i]
+    second, third, shift = marks[0], marks[1], marks[3]
+    token = marks[2] + i * rows
+    first = token - shift
+
+    def lowest(t):
+        low = jnp.where(t >= third, third, jnp.where(t >= second, second, 0))
+        if window:
+            low = jnp.maximum(low, t - (window - 1))
+        return low - shift
+
+    b_lo = lowest(token) // k_block
+    b_hi = (first + rows - 1) // k_block + 1
+    b_a = jnp.clip((lowest(token + rows - 1) + k_block - 1) // k_block, b_lo, b_hi)
+    b_b = jnp.clip((first + 1) // k_block, b_a, b_hi)
 
     def block(masked, b, carry):
         start = pl.multiple_of(b * k_block, k_block)
@@ -576,7 +592,8 @@
         if masked:
             j = start + lax.broadcasted_iota(jnp.int32, (k_block, rows), 0)
             r = first + lax.broadcasted_iota(jnp.int32, (k_block, rows), 1)
-            s = jnp.where((j <= r) & (j >= lo_ref[...]), s, -1e30)
+            low = lowest(token + lax.broadcasted_iota(jnp.int32, (1, rows), 1))
+            s = jnp.where((j <= r) & (j >= low), s, -1e30)
         m_old = m_sc[...]
         m_new = jnp.maximum(m_old, jnp.max(s, axis=0, keepdims=True))
         p = jnp.exp2((s - m_new) * scale)
@@ -587,24 +604,17 @@
         acc_sc[...] = acc_sc[...] * alpha + add
         return carry
 
-    lax.fori_loop(bounds[0, i], bounds[1, i], functools.partial(block, True), 0)
-    lax.fori_loop(bounds[1, i], bounds[2, i], functools.partial(block, False), 0)
-    lax.fori_loop(bounds[2, i], bounds[3, i], functools.partial(block, True), 0)
+    lax.fori_loop(b_lo, b_a, functools.partial(block, True), 0)
+    lax.fori_loop(b_a, b_b, functools.partial(block, False), 0)
+    lax.fori_loop(b_b, b_hi, functools.partial(block, True), 0)
     o_ref[...] = jnp.transpose(acc_sc[...] / l_sc[...]).astype(BF16)
 
 
-def _attend(q, kv, row_lo, first_row, block):
+def _attend(q, kv, marks, window, block):
     total, hd = q.shape
     blocks = total // block
-    lo2 = row_lo.reshape(blocks, block)
-    first = first_row + jnp.arange(blocks, dtype=jnp.int32) * block
-    b_lo = lo2[:, 0] // block
-    b_hi = (first + block - 1) // block + 1
-    b_a = jnp.clip((lo2[:, -1] + block - 1) // block, b_lo, b_hi)
-    b_b = jnp.clip((first + 1) // block, b_a, b_hi)
-    bounds = jnp.stack([b_lo, b_a, b_b, b_hi, first]).astype(jnp.int32)
     return pl.pallas_call(
-        functools.partial(_attend_kernel, hd ** -0.5 * math.log2(math.e), block),
+        functools.partial(_attend_kernel, hd ** -0.5 * math.log2(math.e), block, window),
         name="attend",
         out_shape=jax.ShapeDtypeStruct((total, hd), BF16),
         grid_spec=pltpu.PrefetchScalarGridSpec(
@@ -612,14 +622,13 @@
             grid=(blocks,),
             in_specs=[
                 pl.BlockSpec((block, hd), lambda i, b: (i, 0)),
-                pl.BlockSpec((1, block), lambda i, b: (0, i)),
                 pl.BlockSpec(memory_space=pltpu.VMEM),
             ],
             out_specs=pl.BlockSpec((block, hd), lambda i, b: (i, 0)),
             scratch_shapes=[pltpu.VMEM((1, block), F32), pltpu.VMEM((1, block), F32), pltpu.VMEM((hd, block), F32)],
         ),
         compiler_params=pltpu.CompilerParams(dimension_semantics=("arbitrary",), vmem_limit_bytes=VMEM_LIMIT),
-    )(bounds, q, row_lo.reshape(1, total), kv)
+    )(marks, q, kv)
 
 
 def solution(mesh):
@@ -639,33 +648,28 @@
         inv_freq = ROPE_BASE ** (-jnp.arange(hd // 2, dtype=F32) / (hd // 2))
         angles = positions.astype(F32)[:, None] * inv_freq[None, :]
         tab = jnp.concatenate([jnp.cos(angles), jnp.sin(angles)], axis=1)
-        lane = lax.broadcasted_iota(jnp.int32, (8, 128), 1)
-        counts = jnp.where(lane == 0, jnp.sum(segment_ids < 1), jnp.where(lane == 1, jnp.sum(segment_ids < 2), 0)).astype(F32)
-        token = sp_idx * shard + jnp.arange(shard, dtype=jnp.int32)
+        counts = segment_ids.reshape(2, rows // 2)
 
 
         def pick(w):
-            return lax.optimization_barrier(lax.dynamic_slice_in_dim(w, kv_head, 1, 2).reshape(layers, model, hd))
+            return lax.optimization_barrier(lax.dynamic_slice_in_dim(w, kv_head, 1, 2)).reshape(layers, model, hd)
 
         w_kv = lax.cond(tp_idx % 2 == 0, lambda: pick(w_k), lambda: pick(w_v))
         w_q2 = w_q.reshape(layers, model, hd)
         w_o2 = w_o.reshape(layers, hd, model)
         for layer in range(layers):
             windowed = layer % 2 == 0
-            got = _qkv(layer, windowed, shards, x, g_attn[layer:layer + 1], tab, w_q2, w_kv, counts)
+            got = _qkv(layer, windowed, shards, x, g_attn, tab, w_q2, w_kv, counts)
             q, kv = got[0], got[1]
             if layer == 0:
                 tab = got[2]
-                second, third = got[3][0, 0].astype(jnp.int32), got[3][0, 1].astype(jnp.int32)
-                seg_lo = jnp.where(token >= third, third, jnp.where(token >= second, second, 0))
-            if windowed:
-                shift = (sp_idx - 1) * shard
-                row_lo = jnp.maximum(seg_lo, token - (WINDOW - 1)) - shift
-            else:
-                shift = 0
-                row_lo = seg_lo
-            mixed = _attend(q, kv, row_lo, sp_idx * shard - shift, 512 if windowed else 1024)
-            x = _block(layer, mixed, x, g_mlp[layer:layer + 1], w_o2, w_gate, w_up, w_down)
+                tally = got[3]
+                second, third = jnp.sum(tally[0:2]), jnp.sum(tally[2:4])
+            q_token = sp_idx * shard
+            kv_token = q_token - shard if windowed else 0
+            marks = jnp.stack([second.astype(jnp.int32), third.astype(jnp.int32), q_token, kv_token]).astype(jnp.int32)
+            mixed = _attend(q, kv, marks, WINDOW if windowed else 0, 512 if windowed else 1024)
+            x = _block(layer, mixed, x, g_mlp, w_o2, w_gate, w_up, w_down)
         return x
 
     return jax.shard_map(local_fn, mesh=mesh, in_specs=in_specs, out_specs=row_spec, check_vma=False)

time: 498 us -> 498 us (level)
    another operation x3 -> x1, local copies, waits for them, and re-layouts: 10.5 us -> 9.32 us
where the time goes in v4:
time: 498 us
  Pallas kernels  477 us (96%)
  local copies, waits for them, and re-layouts  15.2 us (3%)
    pallas_call x2, Pallas kernels, _block(): pl.pallas_call(functools.partial(_block_kernel, layer), name=f'block_{lay...  294 us
    pallas_call x2, Pallas kernels, _qkv(): pl.pallas_call(functools.partial(_qkv_kernel, layer, gather_tab, windowed...  136 us
    pallas_call x2, Pallas kernels, _attend(): pl.pallas_call(functools.partial(_attend_kernel, hd ** (-0.5) * math.log2...  46.4 us

profile of v4, /device:TPU:112, one launch (start us, length us, event | category | flops | bytes accessed | tf_op | source)
XLA Modules:
  0.0 497.9 jit_solution(17136313592772544078)
XLA Ops:
  0.0 0.7 convert_element_type.14
  0.7 0.5 multiply_cosine_fusion
  1.2 0.7 pad_maximum_fusion.tab_in
  2.0 12.7 %conditional.1 = (bf16[2,2560,256]{2,1,0:T(8,128)(2,1)}) conditional(s32[]{:T(128)} %convert_element_type.15, (s32[]{:T(128)}, bf16[2,2560,4,256]{3,2,1,0:T(4,128)(2,1)}) %tuple.11, (s32[]{:T(128)}, bf16[2,2560,4,256]{3,2,1,0:T(4,128)(2,1)}) %tuple.12), branch_computations={%region_0.1_spmd, %region_1.2_spmd} | conditional | flops 3 | bytes 26214444 | solution.py:657
  2.0 9.3 %copy.16 = bf16[2,2560,4,256]{3,1,0,2:T(8,128)(2,1)} copy(bf16[2,2560,4,256]{3,2,1,0:T(4,128)(2,1)} %get-tuple-element.35) | data formatting | bytes 20971520 | tf_op jit(solution)/shard_map
  11.3 3.4 constant_dynamic-slice_fusion.1
  14.7 68.3 %qkv_0.1 = (bf16[2048,256]{1,0:T(8,128)(2,1)}, bf16[2,4096,256]{2,1,0:T(8,128)(2,1)}, f32[4,512,256]{2,1,0:T(8,128)}, f32[8,128]{1,0:T(8,128)}) custom-call(bf16[256,2560]{1,0:T(8,128)(2,1)} %x_ref.3, bf16[2,2560]{1,0:T(2,128)(2,1)} %g_ref.6, f32[256,256]{1,0:T(8,128)} %pad_maximum_fusion.tab_in, bf16[2,2560,256]{2,1,0:T(8,128)(2,1)} %bitcast.11, ...), custom_call_target="tpu_custom_call" | custom-call | tf_op jit(solution)/shard_map/qkv_0/pallas_call | solution.py:536
  83.0 1.4 slice_reduce_fusion.1
  85.7 0.6 pad_add_fusion.2
  86.3 14.5 %attend.2.m_hbm = bf16[2048,256]{1,0:T(8,128)(2,1)} custom-call(s32[4]{0:T(128)} %get-tuple-element.38.marks, bf16[2048,256]{1,0:T(8,128)(2,1)} %get-tuple-element.27.q_ref, bf16[2,4096,256]{2,1,0:T(8,128)(2,1)} %get-tuple-element.28.kv_ref), custom_call_target="tpu_custom_call" | custom-call | tf_op jit(solution)/shard_map/attend/pallas_call | solution.py:616
  100.7 0.7 pad_add_fusion.marks
  101.4 147.8 %block_0.1.x_ref = bf16[256,2560]{1,0:T(8,128)(2,1)} custom-call(bf16[2048,256]{1,0:T(8,128)(2,1)} %attend.2.m_hbm, bf16[256,2560]{1,0:T(8,128)(2,1)} %x_ref.3, bf16[2,2560]{1,0:T(2,128)(2,1)} %g_ref.7, bf16[2,256,2560]{2,1,0:T(8,128)(2,1)} %bitcast.9, bf16[2,2560,1280]{2,1,0:T(8,128)(2,1)} %wg_hbm.3, bf16[2,2560,1280]{2,1,0:T(8,128)(2,1)} %wu_hbm.3, ...), custom_call_target="tpu_custom_call" | custom-call | tf_op jit(solution)/shard_map/block_0/pallas_call | solution.py:315
  249.2 67.9 %qkv_1.1 = (bf16[2048,256]{1,0:T(8,128)(2,1)}, bf16[2,8192,256]{2,1,0:T(8,128)(2,1)}) custom-call(bf16[256,2560]{1,0:T(8,128)(2,1)} %block_0.1.x_ref, bf16[2,2560]{1,0:T(2,128)(2,1)} %g_ref.6, f32[4,512,256]{2,1,0:T(8,128)} %get-tuple-element.29.tab_in, bf16[2,2560,256]{2,1,0:T(8,128)(2,1)} %bitcast.12, bf16[2,2560,256]{2,1,0:T(8,128)(2,1)} %get-tuple-element.42.wkv_hbm), custom_call_target="tpu_custom_call" | custom-call | tf_op jit(solution)/shard_map/qkv_1/pallas_call | solution.py:536
  317.1 31.9 %attend.3.m_hbm = bf16[2048,256]{1,0:T(8,128)(2,1)} custom-call(s32[4]{0:T(128)} %pad_add_fusion.marks, bf16[2048,256]{1,0:T(8,128)(2,1)} %get-tuple-element.30.q_ref, bf16[2,8192,256]{2,1,0:T(8,128)(2,1)} %get-tuple-element.31.kv_ref), custom_call_target="tpu_custom_call" | custom-call | tf_op jit(solution)/shard_map/attend/pallas_call | solution.py:616
  349.0 146.4 %block_1.1 = bf16[256,2560]{1,0:T(8,128)(2,1)} custom-call(bf16[2048,256]{1,0:T(8,128)(2,1)} %attend.3.m_hbm, bf16[256,2560]{1,0:T(8,128)(2,1)} %block_0.1.x_ref, bf16[2,2560]{1,0:T(2,128)(2,1)} %g_ref.7, bf16[2,256,2560]{2,1,0:T(8,128)(2,1)} %bitcast.10, bf16[2,2560,1280]{2,1,0:T(8,128)(2,1)} %wg_hbm.3, bf16[2,2560,1280]{2,1,0:T(8,128)(2,1)} %wu_hbm.3, ...), custom_call_target="tpu_custom_call" | custom-call | tf_op jit(solution)/shard_map/block_1/pallas_call | solution.py:315
  495.4 2.5 copy.20
  (1 shorter events, 0.0 us)
